TPU v7x, 32 devices: a whole 2x2x4 slice. The times are simulated.
32 devices in a mesh: groups: 2 (over x), expert: 8 (over z, y), tensor: 2 (over core).
Axes of the slice: x: 2, y: 2, z: 4, core: 2. Of those that a mesh axis runs over, the one named last changes fastest.
Arguments:
- tokens: bfloat16 [128, 6144], P(('groups', 'expert')), parts along dimension 0, may hold values from -6 to 6
- routes: int32 [128, 2], P(('groups', 'expert')), parts along dimension 0, may hold values from 0 to 3, all different within a row; in each aligned block of 8 rows (0 to 7, 8 to 15, ...) at most 5 rows name the same one
- router_logits: float32 [128, 4], P(('groups', 'expert')), parts along dimension 0, may hold values from -9 to 310
- gate_weight: bfloat16 [8, 6144, 512], P('expert', None, 'tensor'), may hold values from -0.078125 to 0.078125
- up_weight: bfloat16 [8, 6144, 512], P('expert', None, 'tensor'), may hold values from -0.078125 to 0.078125
- down_weight: bfloat16 [8, 512, 6144], P('expert', 'tensor'), may hold values from -0.1875 to 0.1875
Outputs:
- layer_out: bfloat16 [128, 6144], P(('groups', 'expert'), 'tensor'), parts along dimension 0
There are 2 independent parts, one for each index of `groups`. A program takes and returns all parts, laid end to end along the dimension named above; an argument that names none is the same for every part. Nothing has to cross between parts.
Inputs may be any that keep to these rules, and one draw needn't show every extreme that they name: `routes`: each row names two different experts. In the rows of one index of expert (aligned blocks of 8 rows) no expert is named more than 5 times, and in every draw some block names some expert exactly 5 times.
All inputs are finite; a program needn't handle non-finite values.
Results may differ from a plain program's by a relative error of at most 0.0049.
Values may be sent and summed in bfloat16 or wider, within the bound.
No kernel may reach another device: no remote copies, remote signals or barrier semaphores. Data moves between devices by JAX's collectives and lax.ppermute only.
A program may use at most 64 MiB of HBM per device.

v0:
```python
import functools

import jax
import jax.numpy as jnp
from jax import lax
from jax.experimental import pallas as pl
from jax.experimental.pallas import tpu as pltpu
from jax.sharding import PartitionSpec as P


AXES = ("expert", "tensor")
VMEM = pl.BlockSpec(memory_space=pltpu.VMEM)
MIB = 1 << 20


def partner_plan(devices):
    if devices == 8:
        return [(2, 6), (4, 5), (3, 7)], 1
    last, *rest = range(1, devices)
    half = len(rest) // 2
    return list(zip(rest[:half], rest[half:])), last


def exchange(x, devices, offsets):
    pairs = [
        (d * 2 + c, (d ^ offsets[c]) * 2 + c) for d in range(devices) for c in range(2)
    ]
    return lax.ppermute(x, AXES, pairs)


def swap_cores(x):
    return lax.ppermute(x, "tensor", [(0, 1), (1, 0)])


def call(kernel, inputs, outs, limit, scratch=(), cost=None):
    return pl.pallas_call(
        kernel,
        out_shape=outs,
        in_specs=[VMEM] * inputs,
        out_specs=jax.tree.map(lambda _: VMEM, outs),
        scratch_shapes=scratch,
        compiler_params=pltpu.CompilerParams(vmem_limit_bytes=limit),
        cost_estimate=cost,
    )


def route_kernel(offsets, segments, routes_ref, logits_ref, out):
    routes, logits = routes_ref[...], logits_ref[...]
    ids = lax.broadcasted_iota(jnp.int32, logits.shape, 1)
    picked = [
        jnp.sum(jnp.where(routes[:, k : k + 1] == ids, logits, 0.0), axis=1, keepdims=True)
        for k in range(2)
    ]
    top = jnp.maximum(picked[0], picked[1])
    raised = [jnp.exp(p - top) for p in picked]
    probs = [r / (raised[0] + raised[1]) for r in raised]
    me, core = lax.axis_index("expert"), lax.axis_index("tensor")
    lane = lax.broadcasted_iota(jnp.int32, out.shape, 1)
    total = jnp.zeros(out.shape, jnp.float32)
    for p, (a, b) in enumerate(offsets):
        expert = (me ^ jnp.where(core == 0, a, b)) // segments
        weight = sum(jnp.where(routes[:, k : k + 1] == expert, probs[k], 0.0) for k in range(2))
        total = jnp.where(lane == p, weight, total)
    out[...] = total


def hidden_kernel(count, *refs):
    blocks, (gate, up, keep, give, x) = refs[:-5], refs[-5:]
    rows, _ = blocks[0].shape
    for i, block in enumerate(blocks):
        x[i * rows : (i + 1) * rows, :] = block[...]
    g = jnp.dot(x[...], gate[0], preferred_element_type=jnp.float32)
    u = jnp.dot(x[...], up[0], preferred_element_type=jnp.float32)
    h = (g / (1.0 + jnp.exp(-g)) * u).astype(jnp.bfloat16)
    cut = (count + 2) * rows
    keep[...] = h[:cut]
    give[:rows, :] = h[:rows]
    give[rows : rows + count * rows, :] = h[cut:]
    give[rows + count * rows :, :] = h[cut - rows : cut]


def down_kernel(count, mine, theirs, down, other, *refs):
    outs, out_half, own, scratch = refs[:count], refs[count], refs[count + 1], refs[count + 2]
    width = down.shape[2]
    half = width // 2
    rows = own.shape[0]
    here = pl.multiple_of(lax.axis_index("tensor") * half, 128)
    chunk = 1024
    for at in range(0, width, chunk):
        y = jnp.dot(mine[...], down[0, :, at : at + chunk], preferred_element_type=jnp.float32)
        y += jnp.dot(theirs[...], other[0, :, at : at + chunk], preferred_element_type=jnp.float32)
        for j in range(count):
            outs[j][:, at : at + chunk] = y[(j + 1) * rows : (j + 2) * rows].astype(jnp.bfloat16)
        scratch[:rows, at : at + chunk] = y[:rows]
        scratch[rows:, at : at + chunk] = y[(count + 1) * rows :]
    own[...] = scratch[:rows, pl.ds(here, half)]
    out_half[...] = scratch[rows:, pl.ds(here, half)].astype(jnp.bfloat16)


def mix_kernel(count, weights, own, *refs):
    back, (keep, give) = refs[:count], refs[count:]
    half = own.shape[1]
    core = lax.axis_index("tensor")
    here = pl.multiple_of(core * half, 128)
    there = pl.multiple_of((1 - core) * half, 128)
    w = [weights[:, p : p + 1] for p in range(count + 1)]
    mine = w[0] * own[...]
    away = None
    for p, ref in enumerate(back):
        mine += w[p + 1] * ref[:, pl.ds(here, half)].astype(jnp.float32)
        part = w[p + 1] * ref[:, pl.ds(there, half)].astype(jnp.float32)
        away = part if away is None else away + part
    keep[...] = mine
    give[...] = away


def last_kernel(column, weights, keep, got, back_half, out):
    w = weights[:, column : column + 1]
    total = keep[...] + got[...] + w * back_half[...].astype(jnp.float32)
    out[...] = total.astype(jnp.bfloat16)


def layer(tokens, routes, logits, gate, up, down):
    rows, width = tokens.shape
    devices = lax.axis_size("expert")
    segments = devices // logits.shape[1]
    plan, last = partner_plan(devices)
    count = len(plan)
    half, hidden = width // 2, gate.shape[2]
    bf16, f32 = jnp.bfloat16, jnp.float32
    S = jax.ShapeDtypeStruct
    mine = []
    for offsets in [*plan, (last, last)]:
        mine.append(exchange(tokens, devices, offsets))
    mine, near = mine[:-1], mine[-1]
    other = swap_cores(down)
    weights = call(
        functools.partial(route_kernel, [(0, 0), *plan, (last, last)], segments),
        2, S((rows, 128), f32), 1 * MIB,
        cost=pl.CostEstimate(flops=4_000_000_000, bytes_accessed=20 * MIB, transcendentals=0),
    )(routes, logits)
    theirs = []
    for m in mine:
        theirs.append(swap_cores(m))
    total, cut = (2 * count + 2) * rows, (count + 2) * rows
    keep, give = call(
        functools.partial(hidden_kernel, count), 2 * count + 4,
        [S((cut, hidden), bf16)] * 2, 14 * MIB, [pltpu.VMEM((total, width), bf16)],
    )(tokens, *mine, near, *theirs, gate, up)
    got = swap_cores(give)
    *outs, out_half, own = call(
        functools.partial(down_kernel, count), 4,
        [S((rows, width), bf16)] * count + [S((rows, half), bf16), S((rows, half), f32)],
        14 * MIB, [pltpu.VMEM((2 * rows, width), f32)],
    )(keep, got, down, other)
    back = []
    for o, offsets in zip([*outs, out_half], [*plan, (last, last)]):
        back.append(exchange(o, devices, offsets))
    back, back_half = back[:-1], back[-1]
    keep, give = call(
        functools.partial(mix_kernel, count), count + 2, [S((rows, half), f32)] * 2, 4 * MIB
    )(weights, own, *back)
    got = swap_cores(give)
    return call(
        functools.partial(last_kernel, count + 1), 4, S((rows, half), bf16), 4 * MIB
    )(weights, keep, got, back_half)


def solution(mesh):
    return jax.shard_map(
        layer,
        mesh=mesh,
        in_specs=(
            P(("groups", "expert"), None),
            P(("groups", "expert"), None),
            P(("groups", "expert"), None),
            P("expert", None, "tensor"),
            P("expert", None, "tensor"),
            P("expert", "tensor", None),
        ),
        out_specs=P(("groups", "expert"), "tensor"),
        check_vma=False,
    )
```

profile of v0, /device:TPU:0, one launch (start us, length us, event | category | flops | bytes accessed | tf_op | source)
XLA Modules:
  0.0 43.2 jit_solution(7976633010642296614)
XLA Ops:
  0.0 0.5 %collective-permute-start.8 = (bf16[1,256,6144]{2,1,0:T(8,128)(2,1)}, bf16[1,256,6144]{2,1,0:T(8,128)(2,1)}, u32[]{:S(2)}, u32[]{:S(2)}) collective-permute-start(bf16[1,256,6144]{2,1,0:T(8,128)(2,1)} %down.1), channel_id=1, source_target_pairs={{0,1},{1,0},{2,3},{3,2},{4,5},{5,4},{6,7},{7,6},{8,9},{9,8},{10,11... | collective-permute-start | bytes 9437192 | tf_op jit(solution)/shard_map/ppermute | solution.py:32
  0.5 2.6 %collective-permute-start = (bf16[8,6144]{1,0:T(8,128)(2,1)}, bf16[8,6144]{1,0:T(8,128)(2,1)S(1)}, u32[]{:S(2)}, u32[]{:S(2)}) collective-permute-start(bf16[8,6144]{1,0:T(8,128)(2,1)} %refs_0_.1), channel_id=1, source_target_pairs={{0,4},{1,13},{2,6},{3,15},{4,0},{5,9},{6,2},{7,11},{8,12},{9,5},{1... | collective-permute-start | bytes 294920 | tf_op jit(solution)/shard_map/ppermute | solution.py:28
  3.1 2.6 %collective-permute-start.1 = (bf16[8,6144]{1,0:T(8,128)(2,1)}, bf16[8,6144]{1,0:T(8,128)(2,1)S(1)}, u32[]{:S(2)}, u32[]{:S(2)}) collective-permute-start(bf16[8,6144]{1,0:T(8,128)(2,1)} %refs_0_.1), channel_id=1, source_target_pairs={{0,8},{1,11},{2,10},{3,9},{4,12},{5,15},{6,14},{7,13},{8,0},{9,3},... | collective-permute-start | bytes 294920 | tf_op jit(solution)/shard_map/ppermute | solution.py:28
  5.6 1.4 %collective-permute-start.2 = (bf16[8,6144]{1,0:T(8,128)(2,1)}, bf16[8,6144]{1,0:T(8,128)(2,1)S(1)}, u32[]{:S(2)}, u32[]{:S(2)}) collective-permute-start(bf16[8,6144]{1,0:T(8,128)(2,1)} %refs_0_.1), channel_id=1, source_target_pairs={{0,6},{1,15},{2,4},{3,13},{4,2},{5,11},{6,0},{7,9},{8,14},{9,7},{1... | collective-permute-start | bytes 294920 | tf_op jit(solution)/shard_map/ppermute | solution.py:28
  7.1 0.5 %collective-permute-start.3 = (bf16[8,6144]{1,0:T(8,128)(2,1)}, bf16[8,6144]{1,0:T(8,128)(2,1)S(1)}, u32[]{:S(2)}, u32[]{:S(2)}) collective-permute-start(bf16[8,6144]{1,0:T(8,128)(2,1)} %refs_0_.1), channel_id=1, source_target_pairs={{0,2},{1,3},{2,0},{3,1},{4,6},{5,7},{6,4},{7,5},{8,10},{9,11},{10,... | collective-permute-start | bytes 294920 | tf_op jit(solution)/shard_map/ppermute | solution.py:28
  7.6 1.2 %collective-permute-start.4 = (bf16[8,6144]{1,0:T(8,128)(2,1)S(1)}, bf16[8,6144]{1,0:T(8,128)(2,1)S(1)}, u32[]{:S(2)}, u32[]{:S(2)}) collective-permute-start(bf16[8,6144]{1,0:T(8,128)(2,1)S(1)} %collective-permute-done.refs_1_), channel_id=1, source_target_pairs={{0,1},{1,0},{2,3},{3,2},{4,5},{5,4},{6,7},{7,6},{8,9},{9,8},{10,11... | collective-permute-start | bytes 294920 | tf_op jit(solution)/shard_map/ppermute | solution.py:32
  8.8 2.6 %collective-permute-done.1.refs_2_ = bf16[8,6144]{1,0:T(8,128)(2,1)S(1)} collective-permute-done((bf16[8,6144]{1,0:T(8,128)(2,1)}, bf16[8,6144]{1,0:T(8,128)(2,1)S(1)}, u32[]{:S(2)}, u32[]{:S(2)}) %collective-permute-start.1) | collective-permute-done | bytes 98336 | tf_op jit(solution)/shard_map/ppermute | solution.py:28
  11.4 2.6 %collective-permute-start.5 = (bf16[8,6144]{1,0:T(8,128)(2,1)S(1)}, bf16[8,6144]{1,0:T(8,128)(2,1)S(1)}, u32[]{:S(2)}, u32[]{:S(2)}) collective-permute-start(bf16[8,6144]{1,0:T(8,128)(2,1)S(1)} %collective-permute-done.1.refs_2_), channel_id=1, source_target_pairs={{0,1},{1,0},{2,3},{3,2},{4,5},{5,4},{6,7},{7,6},{8,9},{9,8},{10,11... | collective-permute-start | bytes 294920 | tf_op jit(solution)/shard_map/ppermute | solution.py:32
  14.0 1.5 %collective-permute-done.3.refs_4_ = bf16[8,6144]{1,0:T(8,128)(2,1)S(1)} collective-permute-done((bf16[8,6144]{1,0:T(8,128)(2,1)}, bf16[8,6144]{1,0:T(8,128)(2,1)S(1)}, u32[]{:S(2)}, u32[]{:S(2)}) %collective-permute-start.3) | collective-permute-done | bytes 98336 | tf_op jit(solution)/shard_map/ppermute | solution.py:28
  15.5 1.9 %copy-done = bf16[1,6144,256]{2,1,0:T(8,128)(2,1)S(1)} copy-done((bf16[1,6144,256]{2,1,0:T(8,128)(2,1)S(1)}, bf16[1,6144,256]{2,1,0:T(8,128)(2,1)}, u32[]{:S(2)}) %copy-start) | copy-done | bytes 3145752
  17.4 1.9 %copy-done.1 = bf16[1,6144,256]{2,1,0:T(8,128)(2,1)S(1)} copy-done((bf16[1,6144,256]{2,1,0:T(8,128)(2,1)S(1)}, bf16[1,6144,256]{2,1,0:T(8,128)(2,1)}, u32[]{:S(2)}) %copy-start.1) | copy-done | bytes 3145752
  19.3 0.9 %copy-done.3 = bf16[8,6144]{1,0:T(8,128)(2,1)S(1)} copy-done((bf16[8,6144]{1,0:T(8,128)(2,1)S(1)}, bf16[8,6144]{1,0:T(8,128)(2,1)}, u32[]{:S(2)}) %copy-start.3) | copy-done | bytes 98328
  20.2 1.2 %shard_map.65 = (bf16[40,256]{1,0:T(8,128)(2,1)S(1)}, bf16[40,256]{1,0:T(8,128)(2,1)S(1)}) custom-call(bf16[8,6144]{1,0:T(8,128)(2,1)S(1)} %copy-done.3, bf16[8,6144]{1,0:T(8,128)(2,1)S(1)} %collective-permute-done.refs_1_, bf16[8,6144]{1,0:T(8,128)(2,1)S(1)} %collective-permute-done.1.refs_2_, bf16[8,6144]{1,0:T(8,128)(2,1)S(1)} %collective-permute-done.2.refs_3_, ...), custom_call_target="tpu_custom_call" | custom-call | tf_op jit(solution)/shard_map/pallas_call | solution.py:146
  21.7 1.0 %collective-permute-done.7.theirs = bf16[40,256]{1,0:T(8,128)(2,1)S(1)} collective-permute-done((bf16[40,256]{1,0:T(8,128)(2,1)S(1)}, bf16[40,256]{1,0:T(8,128)(2,1)S(1)}, u32[]{:S(2)}, u32[]{:S(2)}) %collective-permute-start.7) | collective-permute-done | bytes 20512 | tf_op jit(solution)/shard_map/ppermute | solution.py:32
  22.7 3.1 %shard_map.66 = (bf16[8,6144]{1,0:T(8,128)(2,1)S(1)}, bf16[8,6144]{1,0:T(8,128)(2,1)S(1)}, bf16[8,6144]{1,0:T(8,128)(2,1)S(1)}, bf16[8,3072]{1,0:T(8,128)(2,1)S(1)}, f32[8,3072]{1,0:T(8,128)S(1)}) custom-call(bf16[40,256]{1,0:T(8,128)(2,1)S(1)} %get-tuple-element.14.mine, bf16[40,256]{1,0:T(8,128)(2,1)S(1)} %collective-permute-done.7.theirs, ...), custom_call_target="tpu_custom_call" | custom-call | tf_op jit(solution)/shard_map/pallas_call | solution.py:151
  25.8 2.1 %collective-permute-start.10 = (bf16[8,6144]{1,0:T(8,128)(2,1)S(1)}, bf16[8,6144]{1,0:T(8,128)(2,1)S(1)}, u32[]{:S(2)}, u32[]{:S(2)}) collective-permute-start(bf16[8,6144]{1,0:T(8,128)(2,1)S(1)} %get-tuple-element.18), channel_id=1, source_target_pairs={{0,8},{1,11},{2,10},{3,9},{4,12},{5,15},{6,14},{7,13},{8,0},{9,3},... | collective-permute-start | bytes 294920 | tf_op jit(solution)/shard_map/ppermute | solution.py:28
  27.9 2.0 %collective-permute-start.11 = (bf16[8,6144]{1,0:T(8,128)(2,1)S(1)}, bf16[8,6144]{1,0:T(8,128)(2,1)S(1)}, u32[]{:S(2)}, u32[]{:S(2)}) collective-permute-start(bf16[8,6144]{1,0:T(8,128)(2,1)S(1)} %get-tuple-element.19), channel_id=1, source_target_pairs={{0,6},{1,15},{2,4},{3,13},{4,2},{5,11},{6,0},{7,9},{8,14},{9,7},{1... | collective-permute-start | bytes 294920 | tf_op jit(solution)/shard_map/ppermute | solution.py:28
  29.9 0.8 %collective-permute-start.9 = (bf16[8,6144]{1,0:T(8,128)(2,1)S(1)}, bf16[8,6144]{1,0:T(8,128)(2,1)S(1)}, u32[]{:S(2)}, u32[]{:S(2)}) collective-permute-start(bf16[8,6144]{1,0:T(8,128)(2,1)S(1)} %get-tuple-element.17), channel_id=1, source_target_pairs={{0,4},{1,13},{2,6},{3,15},{4,0},{5,9},{6,2},{7,11},{8,12},{9,5},{1... | collective-permute-start | bytes 294920 | tf_op jit(solution)/shard_map/ppermute | solution.py:28
  30.7 0.3 shard_map.64.weights
  31.0 5.6 %collective-permute-done.10.refs_1_ = bf16[8,6144]{1,0:T(8,128)(2,1)S(1)} collective-permute-done((bf16[8,6144]{1,0:T(8,128)(2,1)S(1)}, bf16[8,6144]{1,0:T(8,128)(2,1)S(1)}, u32[]{:S(2)}, u32[]{:S(2)}) %collective-permute-start.10) | collective-permute-done | bytes 98336 | tf_op jit(solution)/shard_map/ppermute | solution.py:28
  36.6 1.5 %collective-permute-done.9.refs_0_ = bf16[8,6144]{1,0:T(8,128)(2,1)S(1)} collective-permute-done((bf16[8,6144]{1,0:T(8,128)(2,1)S(1)}, bf16[8,6144]{1,0:T(8,128)(2,1)S(1)}, u32[]{:S(2)}, u32[]{:S(2)}) %collective-permute-start.9) | collective-permute-done | bytes 98336 | tf_op jit(solution)/shard_map/ppermute | solution.py:28
  38.4 0.6 %collective-permute-start.13 = (bf16[8,3072]{1,0:T(8,128)(2,1)S(1)}, bf16[8,3072]{1,0:T(8,128)(2,1)S(1)}, u32[]{:S(2)}, u32[]{:S(2)}) collective-permute-start(bf16[8,3072]{1,0:T(8,128)(2,1)S(1)} %get-tuple-element.22), channel_id=1, source_target_pairs={{0,2},{1,3},{2,0},{3,1},{4,6},{5,7},{6,4},{7,5},{8,10},{9,11},{10,... | collective-permute-start | bytes 147464 | tf_op jit(solution)/shard_map/ppermute | solution.py:28
  39.0 3.6 %collective-permute-done.13.back_half = bf16[8,3072]{1,0:T(8,128)(2,1)S(1)} collective-permute-done((bf16[8,3072]{1,0:T(8,128)(2,1)S(1)}, bf16[8,3072]{1,0:T(8,128)(2,1)S(1)}, u32[]{:S(2)}, u32[]{:S(2)}) %collective-permute-start.13) | collective-permute-done | bytes 49184 | tf_op jit(solution)/shard_map/ppermute | solution.py:28
  42.5 0.7 %shard_map.68 = bf16[8,3072]{1,0:T(8,128)(2,1)} custom-call(f32[8,128]{1,0:T(8,128)S(1)} %shard_map.64.weights, f32[8,3072]{1,0:T(8,128)S(1)} %get-tuple-element.20.keep, f32[8,3072]{1,0:T(8,128)S(1)} %collective-permute-done.12.got, bf16[8,3072]{1,0:T(8,128)(2,1)S(1)} %collective-permute-done.13.back_half), custom_call_target="tpu_custom_call" | custom-call | tf_op jit(solution)/shard_map/pallas_call | solution.py:164
  (23 shorter events, 0.5 us)
Async XLA Ops:
  0.0 22.7 %collective-permute-start.8 = (bf16[1,256,6144]{2,1,0:T(8,128)(2,1)}, bf16[1,256,6144]{2,1,0:T(8,128)(2,1)}, u32[]{:S(2)}, u32[]{:S(2)}) collective-permute-start(bf16[1,256,6144]{2,1,0:T(8,128)(2,1)} %down.1), channel_id=1, source_target_pairs={{0,1},{1,0},{2,3},{3,2},{4,5},{5,4},{6,7},{7,6},{8,9},{9,8},{10,11... | collective-permute-start | bytes 9437192 | tf_op jit(solution)/shard_map/ppermute | solution.py:32
  0.5 7.1 %collective-permute-start = (bf16[8,6144]{1,0:T(8,128)(2,1)}, bf16[8,6144]{1,0:T(8,128)(2,1)S(1)}, u32[]{:S(2)}, u32[]{:S(2)}) collective-permute-start(bf16[8,6144]{1,0:T(8,128)(2,1)} %refs_0_.1), channel_id=1, source_target_pairs={{0,4},{1,13},{2,6},{3,15},{4,0},{5,9},{6,2},{7,11},{8,12},{9,5},{1... | collective-permute-start | bytes 294920 | tf_op jit(solution)/shard_map/ppermute | solution.py:28
  3.1 8.4 %collective-permute-start.1 = (bf16[8,6144]{1,0:T(8,128)(2,1)}, bf16[8,6144]{1,0:T(8,128)(2,1)S(1)}, u32[]{:S(2)}, u32[]{:S(2)}) collective-permute-start(bf16[8,6144]{1,0:T(8,128)(2,1)} %refs_0_.1), channel_id=1, source_target_pairs={{0,8},{1,11},{2,10},{3,9},{4,12},{5,15},{6,14},{7,13},{8,0},{9,3},... | collective-permute-start | bytes 294920 | tf_op jit(solution)/shard_map/ppermute | solution.py:28
  5.6 8.3 %collective-permute-start.2 = (bf16[8,6144]{1,0:T(8,128)(2,1)}, bf16[8,6144]{1,0:T(8,128)(2,1)S(1)}, u32[]{:S(2)}, u32[]{:S(2)}) collective-permute-start(bf16[8,6144]{1,0:T(8,128)(2,1)} %refs_0_.1), channel_id=1, source_target_pairs={{0,6},{1,15},{2,4},{3,13},{4,2},{5,11},{6,0},{7,9},{8,14},{9,7},{1... | collective-permute-start | bytes 294920 | tf_op jit(solution)/shard_map/ppermute | solution.py:28
  7.1 8.4 %collective-permute-start.3 = (bf16[8,6144]{1,0:T(8,128)(2,1)}, bf16[8,6144]{1,0:T(8,128)(2,1)S(1)}, u32[]{:S(2)}, u32[]{:S(2)}) collective-permute-start(bf16[8,6144]{1,0:T(8,128)(2,1)} %refs_0_.1), channel_id=1, source_target_pairs={{0,2},{1,3},{2,0},{3,1},{4,6},{5,7},{6,4},{7,5},{8,10},{9,11},{10,... | collective-permute-start | bytes 294920 | tf_op jit(solution)/shard_map/ppermute | solution.py:28
  7.6 7.9 %collective-permute-start.4 = (bf16[8,6144]{1,0:T(8,128)(2,1)S(1)}, bf16[8,6144]{1,0:T(8,128)(2,1)S(1)}, u32[]{:S(2)}, u32[]{:S(2)}) collective-permute-start(bf16[8,6144]{1,0:T(8,128)(2,1)S(1)} %collective-permute-done.refs_1_), channel_id=1, source_target_pairs={{0,1},{1,0},{2,3},{3,2},{4,5},{5,4},{6,7},{7,6},{8,9},{9,8},{10,11... | collective-permute-start | bytes 294920 | tf_op jit(solution)/shard_map/ppermute | solution.py:32
  11.4 4.1 %collective-permute-start.5 = (bf16[8,6144]{1,0:T(8,128)(2,1)S(1)}, bf16[8,6144]{1,0:T(8,128)(2,1)S(1)}, u32[]{:S(2)}, u32[]{:S(2)}) collective-permute-start(bf16[8,6144]{1,0:T(8,128)(2,1)S(1)} %collective-permute-done.1.refs_2_), channel_id=1, source_target_pairs={{0,1},{1,0},{2,3},{3,2},{4,5},{5,4},{6,7},{7,6},{8,9},{9,8},{10,11... | collective-permute-start | bytes 294920 | tf_op jit(solution)/shard_map/ppermute | solution.py:32
  14.0 1.5 %collective-permute-start.6 = (bf16[8,6144]{1,0:T(8,128)(2,1)S(1)}, bf16[8,6144]{1,0:T(8,128)(2,1)S(1)}, u32[]{:S(2)}, u32[]{:S(2)}) collective-permute-start(bf16[8,6144]{1,0:T(8,128)(2,1)S(1)} %collective-permute-done.2.refs_3_), channel_id=1, source_target_pairs={{0,1},{1,0},{2,3},{3,2},{4,5},{5,4},{6,7},{7,6},{8,9},{9,8},{10,11... | collective-permute-start | bytes 294920 | tf_op jit(solution)/shard_map/ppermute | solution.py:32
  15.5 1.9 %copy-start = (bf16[1,6144,256]{2,1,0:T(8,128)(2,1)S(1)}, bf16[1,6144,256]{2,1,0:T(8,128)(2,1)}, u32[]{:S(2)}) copy-start(bf16[1,6144,256]{2,1,0:T(8,128)(2,1)} %refs_8_.1) | copy-start | bytes 9437188
  17.4 1.9 %copy-start.1 = (bf16[1,6144,256]{2,1,0:T(8,128)(2,1)S(1)}, bf16[1,6144,256]{2,1,0:T(8,128)(2,1)}, u32[]{:S(2)}) copy-start(bf16[1,6144,256]{2,1,0:T(8,128)(2,1)} %refs_9_.1) | copy-start | bytes 9437188
  19.3 0.9 %copy-start.3 = (bf16[8,6144]{1,0:T(8,128)(2,1)S(1)}, bf16[8,6144]{1,0:T(8,128)(2,1)}, u32[]{:S(2)}) copy-start(bf16[8,6144]{1,0:T(8,128)(2,1)} %refs_0_.1) | copy-start | bytes 294916
  20.2 1.4 %copy-start.5 = (s32[8,2]{0,1:T(2,128)S(1)}, s32[8,2]{0,1:T(2,128)}, u32[]{:S(2)}) copy-start(s32[8,2]{0,1:T(2,128)} %param.7) | copy-start | bytes 196
  20.2 1.4 %copy-start.4 = (f32[8,4]{0,1:T(4,128)S(1)}, f32[8,4]{0,1:T(4,128)}, u32[]{:S(2)}) copy-start(f32[8,4]{0,1:T(4,128)} %param.8) | copy-start | bytes 388
  20.2 2.5 %copy-start.2 = (bf16[1,256,6144]{2,1,0:T(8,128)(2,1)S(1)}, bf16[1,256,6144]{2,1,0:T(8,128)(2,1)}, u32[]{:S(2)}) copy-start(bf16[1,256,6144]{2,1,0:T(8,128)(2,1)} %down.1) | copy-start | bytes 9437188
  21.4 1.3 %collective-permute-start.7 = (bf16[40,256]{1,0:T(8,128)(2,1)S(1)}, bf16[40,256]{1,0:T(8,128)(2,1)S(1)}, u32[]{:S(2)}, u32[]{:S(2)}) collective-permute-start(bf16[40,256]{1,0:T(8,128)(2,1)S(1)} %get-tuple-element.15), channel_id=1, source_target_pairs={{0,1},{1,0},{2,3},{3,2},{4,5},{5,4},{6,7},{7,6},{8,9},{9,8},{10,11... | collective-permute-start | bytes 61448 | tf_op jit(solution)/shard_map/ppermute | solution.py:32
  25.8 10.8 %collective-permute-start.10 = (bf16[8,6144]{1,0:T(8,128)(2,1)S(1)}, bf16[8,6144]{1,0:T(8,128)(2,1)S(1)}, u32[]{:S(2)}, u32[]{:S(2)}) collective-permute-start(bf16[8,6144]{1,0:T(8,128)(2,1)S(1)} %get-tuple-element.18), channel_id=1, source_target_pairs={{0,8},{1,11},{2,10},{3,9},{4,12},{5,15},{6,14},{7,13},{8,0},{9,3},... | collective-permute-start | bytes 294920 | tf_op jit(solution)/shard_map/ppermute | solution.py:28
  27.9 8.7 %collective-permute-start.11 = (bf16[8,6144]{1,0:T(8,128)(2,1)S(1)}, bf16[8,6144]{1,0:T(8,128)(2,1)S(1)}, u32[]{:S(2)}, u32[]{:S(2)}) collective-permute-start(bf16[8,6144]{1,0:T(8,128)(2,1)S(1)} %get-tuple-element.19), channel_id=1, source_target_pairs={{0,6},{1,15},{2,4},{3,13},{4,2},{5,11},{6,0},{7,9},{8,14},{9,7},{1... | collective-permute-start | bytes 294920 | tf_op jit(solution)/shard_map/ppermute | solution.py:28
  29.9 8.3 %collective-permute-start.9 = (bf16[8,6144]{1,0:T(8,128)(2,1)S(1)}, bf16[8,6144]{1,0:T(8,128)(2,1)S(1)}, u32[]{:S(2)}, u32[]{:S(2)}) collective-permute-start(bf16[8,6144]{1,0:T(8,128)(2,1)S(1)} %get-tuple-element.17), channel_id=1, source_target_pairs={{0,4},{1,13},{2,6},{3,15},{4,0},{5,9},{6,2},{7,11},{8,12},{9,5},{1... | collective-permute-start | bytes 294920 | tf_op jit(solution)/shard_map/ppermute | solution.py:28
  38.3 4.2 %collective-permute-start.12 = (f32[8,3072]{1,0:T(8,128)S(1)}, f32[8,3072]{1,0:T(8,128)S(1)}, u32[]{:S(2)}, u32[]{:S(2)}) collective-permute-start(f32[8,3072]{1,0:T(8,128)S(1)} %get-tuple-element.21), channel_id=1, source_target_pairs={{0,1},{1,0},{2,3},{3,2},{4,5},{5,4},{6,7},{7,6},{8,9},{9,8},{10,11... | collective-permute-start | bytes 294920 | tf_op jit(solution)/shard_map/ppermute | solution.py:32
  38.4 4.2 %collective-permute-start.13 = (bf16[8,3072]{1,0:T(8,128)(2,1)S(1)}, bf16[8,3072]{1,0:T(8,128)(2,1)S(1)}, u32[]{:S(2)}, u32[]{:S(2)}) collective-permute-start(bf16[8,3072]{1,0:T(8,128)(2,1)S(1)} %get-tuple-element.22), channel_id=1, source_target_pairs={{0,2},{1,3},{2,0},{3,1},{4,6},{5,7},{6,4},{7,5},{8,10},{9,11},{10,... | collective-permute-start | bytes 147464 | tf_op jit(solution)/shard_map/ppermute | solution.py:28
where the time goes:
time: 43.5 us; the launch traced here: 43.2 us
  starting transfers between devices  17.1 us (39%)
  waiting for transfers between devices  15.8 us (36%)
  Pallas kernels  5.42 us (12%)
  local copies, waits for them, and re-layouts  4.84 us (11%)
    ppermute x8, waiting for transfers between devices, exchange(): return lax.ppermute(x, AXES, pairs)  14.9 us
    ppermute x8, starting transfers between devices, exchange(): return lax.ppermute(x, AXES, pairs)  12.6 us
    unnamed x14, local copies, waits for them, and re-layouts  4.84 us
    ppermute x6, starting transfers between devices, swap_cores(): return lax.ppermute(x, 'tensor', [(0, 1), (1, 0)])  4.5 us
    pallas_call x1, Pallas kernels, layer(): call(functools.partial(down_kernel, count), 4, [S((rows, width), bf16)] *...  3.08 us
    pallas_call x1, Pallas kernels, layer(): call(functools.partial(hidden_kernel, count), 2 * count + 4, [S((cut, hid...  1.21 us
    ppermute x6, waiting for transfers between devices, swap_cores(): return lax.ppermute(x, 'tensor', [(0, 1), (1, 0)])  0.96 us
  transfers between devices with their start and end apart: 14, of which 6 were waited for; matrix products, arithmetic and copies ran while one was open for 0% of the time, Pallas kernels for 3%

commit v1 on v0

v1 whole, which is shorter than its diff:
```python
import functools

import jax
import jax.numpy as jnp
from jax import lax
from jax.experimental import pallas as pl
from jax.experimental.pallas import tpu as pltpu
from jax.sharding import PartitionSpec as P


CAP = 5
BASE = 4
AXES = ("expert", "tensor")
VMEM = pl.BlockSpec(memory_space=pltpu.VMEM)
MIB = 1 << 20
F32, BF16 = jnp.float32, jnp.bfloat16


def partner_plan(devices):
    if devices == 8:
        return [(2, 6), (4, 5), (3, 7)], 1
    last, *rest = range(1, devices)
    half = len(rest) // 2
    return list(zip(rest[:half], rest[half:])), last


def exchange(x, devices, offsets):
    pairs = [
        (d * 2 + c, (d ^ offsets[c]) * 2 + c) for d in range(devices) for c in range(2)
    ]
    return lax.ppermute(x, AXES, pairs)


def swap_cores(x):
    return lax.ppermute(x, "tensor", [(0, 1), (1, 0)])


def call(kernel, inputs, outs, limit, scratch=(), cost=None):
    return pl.pallas_call(
        kernel,
        out_shape=outs,
        in_specs=[VMEM] * inputs,
        out_specs=jax.tree.map(lambda _: VMEM, outs),
        scratch_shapes=scratch,
        compiler_params=pltpu.CompilerParams(vmem_limit_bytes=limit),
        cost_estimate=cost,
    )


def expert_at(offsets, segments):
    me, core = lax.axis_index("expert"), lax.axis_index("tensor")
    return (me ^ jnp.where(core == 0, offsets[0], offsets[1])) // segments


def unpack(ref, scratch):
    width = scratch.shape[1]
    piece = width // BASE
    scratch[BASE:, :] = jnp.zeros((scratch.shape[0] - BASE, width), F32)
    scratch[:BASE, :] = ref[:, :width].astype(F32)
    beside = ref[:, width:].astype(F32)
    for q in range(BASE):
        scratch[BASE:CAP, q * piece : (q + 1) * piece] = beside[q : q + 1]
    return scratch[...].astype(BF16)


def number_kernel(experts, routes, out):
    rows = routes.shape[1]
    shape, square = (experts, rows), (rows, rows)
    expert = lax.broadcasted_iota(jnp.int32, shape, 0)
    hot = [jnp.where(routes[k : k + 1, :] == expert, 1.0, 0.0) for k in range(2)]
    before = lax.broadcasted_iota(jnp.int32, square, 0) < lax.broadcasted_iota(jnp.int32, square, 1)
    earlier = jnp.dot(
        (hot[0] + hot[1]).astype(BF16), jnp.where(before, 1.0, 0.0).astype(BF16), preferred_element_type=F32
    )
    for k in range(2):
        slot = jnp.sum(hot[k] * earlier, axis=0, keepdims=True)
        out[k : k + 1, :] = routes[k : k + 1, :] * rows + slot.astype(jnp.int32)


def select_kernel(segments, *refs):
    slots, out = refs[:-1], refs[-1]
    rows = out.shape[1]
    here = lax.axis_index("expert") // segments * rows
    here += lax.broadcasted_iota(jnp.int32, (rows, rows), 0)
    for i, ref in enumerate(slots):
        pick = (ref[0:1, :] == here) | (ref[1:2, :] == here)
        out[i * rows : (i + 1) * rows, :] = jnp.where(pick, 1.0, 0.0).astype(BF16)


def route_kernel(dense, packed, segments, routes_ref, logits_ref, out, coefs):
    routes, logits = routes_ref[...], logits_ref[...]
    rows = routes.shape[0]
    ids = lax.broadcasted_iota(jnp.int32, logits.shape, 1)
    picked = [
        jnp.sum(jnp.where(routes[:, k : k + 1] == ids, logits, 0.0), axis=1, keepdims=True)
        for k in range(2)
    ]
    top = jnp.maximum(picked[0], picked[1])
    raised = [jnp.exp(p - top) for p in picked]
    probs = [r / (raised[0] + raised[1]) for r in raised]

    def chosen(offsets):
        expert = expert_at(offsets, segments)
        hits = [routes[:, k : k + 1] == expert for k in range(2)]
        return hits[0] | hits[1], jnp.where(hits[0], probs[0], 0.0) + jnp.where(hits[1], probs[1], 0.0)

    lane = lax.broadcasted_iota(jnp.int32, out.shape, 1)
    total = jnp.zeros(out.shape, F32)
    for p, offsets in enumerate(dense):
        total = jnp.where(lane == p, chosen(offsets)[1], total)
    out[...] = total
    shape = (rows, coefs.shape[1])
    lane = lax.broadcasted_iota(jnp.int32, shape, 1)
    marks = jnp.zeros(shape, F32)
    value = jnp.zeros(shape, F32)
    for p, offsets in enumerate(packed):
        hit, weight = chosen(offsets)
        here = lane // rows == p
        marks = jnp.where(here & hit, 1.0, marks)
        value = jnp.where(here, weight, value)
    square = (rows, rows)
    before = lax.broadcasted_iota(jnp.int32, square, 1) < lax.broadcasted_iota(jnp.int32, square, 0)
    slot = jnp.dot(
        jnp.where(before, 1.0, 0.0).astype(BF16), marks.astype(BF16), preferred_element_type=F32
    )
    value = jnp.where((slot == (lane % rows).astype(F32)) & (marks > 0), value, 0.0)
    high = value.astype(BF16)
    coefs[:rows, :] = high
    coefs[rows:, :] = (value - high.astype(F32)).astype(BF16)


def hidden_kernel(count, *refs):
    blocks, (gate, up, keep, give, x) = refs[:-5], refs[-5:]
    rows, _ = blocks[0].shape
    for i, block in enumerate(blocks):
        x[i * rows : (i + 1) * rows, :] = block[...]
    g = jnp.dot(x[...], gate[0], preferred_element_type=jnp.float32)
    u = jnp.dot(x[...], up[0], preferred_element_type=jnp.float32)
    h = (g / (1.0 + jnp.exp(-g)) * u).astype(jnp.bfloat16)
    cut = (count + 2) * rows
    keep[...] = h[:cut]
    give[:rows, :] = h[:rows]
    give[rows : rows + count * rows, :] = h[cut:]
    give[rows + count * rows :, :] = h[cut - rows : cut]


def down_kernel(count, mine, theirs, picks, down, other, *refs):
    outs, out_half, own = refs[:count], refs[count], refs[count + 1]
    left, right, scratch, *spares = refs[count + 2 :]
    width = down.shape[2]
    half, piece = width // 2, width // BASE
    rows = own.shape[0]
    here = pl.multiple_of(lax.axis_index("tensor") * half, 128)
    for hidden, ref in ((mine, left), (theirs, right)):
        ref[:rows, :] = hidden[:rows, :]
        for i in range(count):
            at = slice((i + 1) * rows, (i + 2) * rows)
            pick = picks[i * rows : (i + 1) * rows, :]
            ref[at, :] = jnp.dot(pick, hidden[at, :], preferred_element_type=F32).astype(BF16)
        ref[(count + 1) * rows :, :] = hidden[(count + 1) * rows :, :]
    for q in range(BASE):
        at = slice(q * piece, (q + 1) * piece)
        y = jnp.dot(left[...], down[0, :, at], preferred_element_type=F32)
        y += jnp.dot(right[...], other[0, :, at], preferred_element_type=F32)
        scratch[:rows, at] = y[:rows]
        scratch[rows:, at] = y[(count + 1) * rows :]
        for i in range(count):
            row = (i + 1) * rows
            outs[i][:, at] = y[row : row + BASE].astype(BF16)
            spares[i][q : q + 1, :] = y[row + BASE : row + CAP]
    own[...] = scratch[:rows, pl.ds(here, half)]
    out_half[...] = scratch[rows:, pl.ds(here, half)].astype(BF16)
    for out, spare in zip(outs, spares):
        out[:, width:] = spare[...].astype(BF16)


def mix_kernel(count, weights, coefs, own, *refs):
    back = refs[:count]
    keep, give, stack, total, *spreads = refs[count:]
    rows, half = own.shape
    core = lax.axis_index("tensor")
    here = pl.multiple_of(core * half, 128)
    there = pl.multiple_of((1 - core) * half, 128)
    for i, (block, spread) in enumerate(zip(back, spreads)):
        stack[i * rows : (i + 1) * rows, :] = unpack(block, spread)
    mixed = jnp.dot(coefs[...], stack[...], preferred_element_type=F32)
    total[...] = mixed[:rows] + mixed[rows:]
    keep[...] = total[:, pl.ds(here, half)] + weights[:, 0:1] * own[...]
    give[...] = total[:, pl.ds(there, half)]


def last_kernel(weights, keep, got, back_half, out):
    total = keep[...] + got[...] + weights[:, 1:2] * back_half[...].astype(F32)
    out[...] = total.astype(BF16)


def layer(tokens, routes, logits, gate, up, down):
    rows, width = tokens.shape
    devices = lax.axis_size("expert")
    segments = devices // logits.shape[1]
    plan, last = partner_plan(devices)
    count = len(plan)
    half, hidden = width // 2, gate.shape[2]
    bf16, f32 = jnp.bfloat16, jnp.float32
    S = jax.ShapeDtypeStruct
    mine = []
    for offsets in [*plan, (last, last)]:
        mine.append(exchange(tokens, devices, offsets))
    mine, near = mine[:-1], mine[-1]
    other = swap_cores(down)
    hint = pl.CostEstimate(flops=4_000_000_000, bytes_accessed=20 * MIB, transcendentals=0)
    numbers = call(
        functools.partial(number_kernel, logits.shape[1]), 1, S((2, rows), jnp.int32), 1 * MIB, cost=hint
    )(routes.T)
    routed = []
    for offsets in plan:
        routed.append(exchange(numbers, devices, offsets))
    weights, coefs = call(
        functools.partial(route_kernel, [(0, 0), (last, last)], plan, segments), 2,
        [S((rows, 128), f32), S((2 * rows, count * rows), bf16)], 1 * MIB,
    )(routes, logits)
    picks = call(functools.partial(select_kernel, segments), count, S((count * rows, rows), bf16), 1 * MIB)(*routed)
    theirs = []
    for m in mine:
        theirs.append(swap_cores(m))
    total, cut = (2 * count + 2) * rows, (count + 2) * rows
    keep, give = call(
        functools.partial(hidden_kernel, count), 2 * count + 4,
        [S((cut, hidden), bf16)] * 2, 14 * MIB, [pltpu.VMEM((total, width), bf16)],
    )(tokens, *mine, near, *theirs, gate, up)
    got = swap_cores(give)
    slots = S((BASE, width * CAP // BASE), bf16)
    spare, spread = pltpu.VMEM((BASE, width // BASE), f32), pltpu.VMEM((rows, width), f32)
    *outs, out_half, own = call(
        functools.partial(down_kernel, count), 5,
        [slots] * count + [S((rows, half), bf16), S((rows, half), f32)], 14 * MIB,
        [pltpu.VMEM((cut, hidden), bf16)] * 2 + [pltpu.VMEM((2 * rows, width), f32)] + [spare] * count,
    )(keep, got, picks, down, other)
    back = []
    for o, offsets in zip([*outs, out_half], [*plan, (last, last)]):
        back.append(exchange(o, devices, offsets))
    back, back_half = back[:-1], back[-1]
    keep, give = call(
        functools.partial(mix_kernel, count), count + 3, [S((rows, half), f32)] * 2,
        4 * MIB + count * MIB,
        [pltpu.VMEM((count * rows, width), bf16), spread] + [spread] * count,
    )(weights, coefs, own, *back)
    got = swap_cores(give)
    return call(last_kernel, 4, S((rows, half), bf16), 4 * MIB)(weights, keep, got, back_half)


def solution(mesh):
    return jax.shard_map(
        layer,
        mesh=mesh,
        in_specs=(
            P(("groups", "expert"), None),
            P(("groups", "expert"), None),
            P(("groups", "expert"), None),
            P("expert", None, "tensor"),
            P("expert", None, "tensor"),
            P("expert", "tensor", None),
        ),
        out_specs=P(("groups", "expert"), "tensor"),
        check_vma=False,
    )
```

time: 43.5 us -> 46.1 us (1.060)
  starting transfers between devices: 17.1 us -> 21.9 us
  Pallas kernels: 5.42 us -> 3.94 us
  waiting for transfers between devices: 15.8 us -> 15.1 us
    ppermute x8 -> x11, starting transfers between devices: 12.6 us -> 17.4 us  [exchange(): return lax.ppermute(x, AXES, pairs)]
    pallas_call x4 -> x6, Pallas kernels: 4.2 us -> 2.73 us  [the longest x1 1.3 us: layer(): call(functools.partial(down_kernel, count), 5, [slots] * count + [S((rows...]
    ppermute x6, waiting for transfers between devices: 0.96 us -> 0.02 us  [swap_cores(): return lax.ppermute(x, 'tensor', [(0, 1), (1, 0)])]
    ppermute x8 -> x11, waiting for transfers between devices: 14.9 us -> 15.1 us  [exchange(): return lax.ppermute(x, AXES, pairs)]
  transfers between devices with their start and end apart: 14 -> 17, of which waited for: 6 -> 6; matrix products, arithmetic and copies ran while one was open for 0% -> 0% of each run, Pallas kernels for 3% -> 4%
where the time goes in v1:
time: 46.1 us; the launch traced here: 45.9 us
  starting transfers between devices  21.9 us (48%)
  waiting for transfers between devices  15.1 us (33%)
  local copies, waits for them, and re-layouts  4.84 us (10%)
  Pallas kernels  3.94 us (9%)
    ppermute x11, starting transfers between devices, exchange(): return lax.ppermute(x, AXES, pairs)  17.4 us
    ppermute x11, waiting for transfers between devices, exchange(): return lax.ppermute(x, AXES, pairs)  15.1 us
    unnamed x14, local copies, waits for them, and re-layouts  4.84 us
    ppermute x6, starting transfers between devices, swap_cores(): return lax.ppermute(x, 'tensor', [(0, 1), (1, 0)])  4.5 us
    pallas_call x1, Pallas kernels, layer(): call(functools.partial(down_kernel, count), 5, [slots] * count + [S((rows...  1.3 us
    pallas_call x1, Pallas kernels, layer(): call(functools.partial(hidden_kernel, count), 2 * count + 4, [S((cut, hid...  1.21 us
  transfers between devices with their start and end apart: 17, of which 6 were waited for; matrix products, arithmetic and copies ran while one was open for 0% of the time, Pallas kernels for 4%

profile of v1, /device:TPU:0, one launch (start us, length us, event | category | flops | bytes accessed | tf_op | source)
XLA Modules:
  0.0 45.9 jit_solution(17362122882424682002)
XLA Ops:
  0.5 2.6 %collective-permute-start = (bf16[8,6144]{1,0:T(8,128)(2,1)}, bf16[8,6144]{1,0:T(8,128)(2,1)S(1)}, u32[]{:S(2)}, u32[]{:S(2)}) collective-permute-start(bf16[8,6144]{1,0:T(8,128)(2,1)} %refs_0_.1), channel_id=1, source_target_pairs={{0,4},{1,13},{2,6},{3,15},{4,0},{5,9},{6,2},{7,11},{8,12},{9,5},{1... | collective-permute-start | bytes 294920 | tf_op jit(solution)/shard_map/ppermute | solution.py:31
  3.1 2.6 %collective-permute-start.1 = (bf16[8,6144]{1,0:T(8,128)(2,1)}, bf16[8,6144]{1,0:T(8,128)(2,1)S(1)}, u32[]{:S(2)}, u32[]{:S(2)}) collective-permute-start(bf16[8,6144]{1,0:T(8,128)(2,1)} %refs_0_.1), channel_id=1, source_target_pairs={{0,8},{1,11},{2,10},{3,9},{4,12},{5,15},{6,14},{7,13},{8,0},{9,3},... | collective-permute-start | bytes 294920 | tf_op jit(solution)/shard_map/ppermute | solution.py:31
  5.6 1.4 %collective-permute-start.2 = (bf16[8,6144]{1,0:T(8,128)(2,1)}, bf16[8,6144]{1,0:T(8,128)(2,1)S(1)}, u32[]{:S(2)}, u32[]{:S(2)}) collective-permute-start(bf16[8,6144]{1,0:T(8,128)(2,1)} %refs_0_.1), channel_id=1, source_target_pairs={{0,6},{1,15},{2,4},{3,13},{4,2},{5,11},{6,0},{7,9},{8,14},{9,7},{1... | collective-permute-start | bytes 294920 | tf_op jit(solution)/shard_map/ppermute | solution.py:31
  7.1 0.5 %collective-permute-start.3 = (bf16[8,6144]{1,0:T(8,128)(2,1)}, bf16[8,6144]{1,0:T(8,128)(2,1)S(1)}, u32[]{:S(2)}, u32[]{:S(2)}) collective-permute-start(bf16[8,6144]{1,0:T(8,128)(2,1)} %refs_0_.1), channel_id=1, source_target_pairs={{0,2},{1,3},{2,0},{3,1},{4,6},{5,7},{6,4},{7,5},{8,10},{9,11},{10,... | collective-permute-start | bytes 294920 | tf_op jit(solution)/shard_map/ppermute | solution.py:31
  7.6 1.2 %collective-permute-start.4 = (bf16[8,6144]{1,0:T(8,128)(2,1)S(1)}, bf16[8,6144]{1,0:T(8,128)(2,1)S(1)}, u32[]{:S(2)}, u32[]{:S(2)}) collective-permute-start(bf16[8,6144]{1,0:T(8,128)(2,1)S(1)} %collective-permute-done.refs_1_), channel_id=1, source_target_pairs={{0,1},{1,0},{2,3},{3,2},{4,5},{5,4},{6,7},{7,6},{8,9},{9,8},{10,11... | collective-permute-start | bytes 294920 | tf_op jit(solution)/shard_map/ppermute | solution.py:35
  8.8 2.6 %collective-permute-done.1.refs_2_ = bf16[8,6144]{1,0:T(8,128)(2,1)S(1)} collective-permute-done((bf16[8,6144]{1,0:T(8,128)(2,1)}, bf16[8,6144]{1,0:T(8,128)(2,1)S(1)}, u32[]{:S(2)}, u32[]{:S(2)}) %collective-permute-start.1) | collective-permute-done | bytes 98336 | tf_op jit(solution)/shard_map/ppermute | solution.py:31
  11.4 2.6 %collective-permute-start.5 = (bf16[8,6144]{1,0:T(8,128)(2,1)S(1)}, bf16[8,6144]{1,0:T(8,128)(2,1)S(1)}, u32[]{:S(2)}, u32[]{:S(2)}) collective-permute-start(bf16[8,6144]{1,0:T(8,128)(2,1)S(1)} %collective-permute-done.1.refs_2_), channel_id=1, source_target_pairs={{0,1},{1,0},{2,3},{3,2},{4,5},{5,4},{6,7},{7,6},{8,9},{9,8},{10,11... | collective-permute-start | bytes 294920 | tf_op jit(solution)/shard_map/ppermute | solution.py:35
  14.0 1.5 %collective-permute-done.3.refs_4_ = bf16[8,6144]{1,0:T(8,128)(2,1)S(1)} collective-permute-done((bf16[8,6144]{1,0:T(8,128)(2,1)}, bf16[8,6144]{1,0:T(8,128)(2,1)S(1)}, u32[]{:S(2)}, u32[]{:S(2)}) %collective-permute-start.3) | collective-permute-done | bytes 98336 | tf_op jit(solution)/shard_map/ppermute | solution.py:31
  15.5 1.9 %copy-done = bf16[1,6144,256]{2,1,0:T(8,128)(2,1)S(1)} copy-done((bf16[1,6144,256]{2,1,0:T(8,128)(2,1)S(1)}, bf16[1,6144,256]{2,1,0:T(8,128)(2,1)}, u32[]{:S(2)}) %copy-start) | copy-done | bytes 3145752
  17.4 1.9 %copy-done.1 = bf16[1,6144,256]{2,1,0:T(8,128)(2,1)S(1)} copy-done((bf16[1,6144,256]{2,1,0:T(8,128)(2,1)S(1)}, bf16[1,6144,256]{2,1,0:T(8,128)(2,1)}, u32[]{:S(2)}) %copy-start.1) | copy-done | bytes 3145752
  19.3 0.9 %copy-done.3 = bf16[8,6144]{1,0:T(8,128)(2,1)S(1)} copy-done((bf16[8,6144]{1,0:T(8,128)(2,1)S(1)}, bf16[8,6144]{1,0:T(8,128)(2,1)}, u32[]{:S(2)}) %copy-start.3) | copy-done | bytes 98328
  20.2 1.2 %shard_map.65 = (bf16[40,256]{1,0:T(8,128)(2,1)S(1)}, bf16[40,256]{1,0:T(8,128)(2,1)S(1)}) custom-call(bf16[8,6144]{1,0:T(8,128)(2,1)S(1)} %copy-done.3, bf16[8,6144]{1,0:T(8,128)(2,1)S(1)} %collective-permute-done.refs_1_, bf16[8,6144]{1,0:T(8,128)(2,1)S(1)} %collective-permute-done.1.refs_2_, bf16[8,6144]{1,0:T(8,128)(2,1)S(1)} %collective-permute-done.2.refs_3_, ...), custom_call_target="tpu_custom_call" | custom-call | tf_op jit(solution)/shard_map/pallas_call | solution.py:227
  21.7 1.3 %collective-permute-start.10 = (s32[2,8]{1,0:T(2,128)S(1)}, s32[2,8]{1,0:T(2,128)S(1)}, u32[]{:S(2)}, u32[]{:S(2)}) collective-permute-start(s32[2,8]{1,0:T(2,128)S(1)} %shard_map.66), channel_id=1, source_target_pairs={{0,6},{1,15},{2,4},{3,13},{4,2},{5,11},{6,0},{7,9},{8,14},{9,7},{1... | collective-permute-start | bytes 200 | tf_op jit(solution)/shard_map/ppermute | solution.py:31
  23.0 1.2 %collective-permute-start.8 = (s32[2,8]{1,0:T(2,128)S(1)}, s32[2,8]{1,0:T(2,128)S(1)}, u32[]{:S(2)}, u32[]{:S(2)}) collective-permute-start(s32[2,8]{1,0:T(2,128)S(1)} %shard_map.66), channel_id=1, source_target_pairs={{0,4},{1,13},{2,6},{3,15},{4,0},{5,9},{6,2},{7,11},{8,12},{9,5},{1... | collective-permute-start | bytes 200 | tf_op jit(solution)/shard_map/ppermute | solution.py:31
  24.1 2.7 %collective-permute-start.9 = (s32[2,8]{1,0:T(2,128)S(1)}, s32[2,8]{1,0:T(2,128)S(1)}, u32[]{:S(2)}, u32[]{:S(2)}) collective-permute-start(s32[2,8]{1,0:T(2,128)S(1)} %shard_map.66), channel_id=1, source_target_pairs={{0,8},{1,11},{2,10},{3,9},{4,12},{5,15},{6,14},{7,13},{8,0},{9,3},... | collective-permute-start | bytes 200 | tf_op jit(solution)/shard_map/ppermute | solution.py:31
  26.8 1.8 %collective-permute-done.9.refs_1_ = s32[2,8]{1,0:T(2,128)S(1)} collective-permute-done((s32[2,8]{1,0:T(2,128)S(1)}, s32[2,8]{1,0:T(2,128)S(1)}, u32[]{:S(2)}, u32[]{:S(2)}) %collective-permute-start.9) | collective-permute-done | bytes 96 | tf_op jit(solution)/shard_map/ppermute | solution.py:31
  28.7 1.3 %shard_map.68 = (bf16[4,7680]{1,0:T(4,128)(2,1)S(1)}, bf16[4,7680]{1,0:T(4,128)(2,1)S(1)}, bf16[4,7680]{1,0:T(4,128)(2,1)S(1)}, bf16[8,3072]{1,0:T(8,128)(2,1)S(1)}, f32[8,3072]{1,0:T(8,128)S(1)}) custom-call(bf16[40,256]{1,0:T(8,128)(2,1)S(1)} %get-tuple-element.18.mine, bf16[40,256]{1,0:T(8,128)(2,1)S(1)} %collective-permute-done.7.theirs, ...), custom_call_target="tpu_custom_call" | custom-call | tf_op jit(solution)/shard_map/pallas_call | solution.py:234
  30.0 1.0 %collective-permute-start.12 = (bf16[4,7680]{1,0:T(4,128)(2,1)S(1)}, bf16[4,7680]{1,0:T(4,128)(2,1)S(1)}, u32[]{:S(2)}, u32[]{:S(2)}) collective-permute-start(bf16[4,7680]{1,0:T(4,128)(2,1)S(1)} %get-tuple-element.21), channel_id=1, source_target_pairs={{0,4},{1,13},{2,6},{3,15},{4,0},{5,9},{6,2},{7,11},{8,12},{9,5},{1... | collective-permute-start | bytes 184328 | tf_op jit(solution)/shard_map/ppermute | solution.py:31
  31.0 2.9 %collective-permute-start.13 = (bf16[4,7680]{1,0:T(4,128)(2,1)S(1)}, bf16[4,7680]{1,0:T(4,128)(2,1)S(1)}, u32[]{:S(2)}, u32[]{:S(2)}) collective-permute-start(bf16[4,7680]{1,0:T(4,128)(2,1)S(1)} %get-tuple-element.22), channel_id=1, source_target_pairs={{0,8},{1,11},{2,10},{3,9},{4,12},{5,15},{6,14},{7,13},{8,0},{9,3},... | collective-permute-start | bytes 184328 | tf_op jit(solution)/shard_map/ppermute | solution.py:31
  33.9 1.0 %collective-permute-start.14 = (bf16[4,7680]{1,0:T(4,128)(2,1)S(1)}, bf16[4,7680]{1,0:T(4,128)(2,1)S(1)}, u32[]{:S(2)}, u32[]{:S(2)}) collective-permute-start(bf16[4,7680]{1,0:T(4,128)(2,1)S(1)} %get-tuple-element.23), channel_id=1, source_target_pairs={{0,6},{1,15},{2,4},{3,13},{4,2},{5,11},{6,0},{7,9},{8,14},{9,7},{1... | collective-permute-start | bytes 184328 | tf_op jit(solution)/shard_map/ppermute | solution.py:31
  35.4 1.1 %collective-permute-done.13.refs_1_ = bf16[4,7680]{1,0:T(4,128)(2,1)S(1)} collective-permute-done((bf16[4,7680]{1,0:T(4,128)(2,1)S(1)}, bf16[4,7680]{1,0:T(4,128)(2,1)S(1)}, u32[]{:S(2)}, u32[]{:S(2)}) %collective-permute-start.13) | collective-permute-done | bytes 61472 | tf_op jit(solution)/shard_map/ppermute | solution.py:31
  36.5 4.2 %collective-permute-done.14.refs_2_ = bf16[4,7680]{1,0:T(4,128)(2,1)S(1)} collective-permute-done((bf16[4,7680]{1,0:T(4,128)(2,1)S(1)}, bf16[4,7680]{1,0:T(4,128)(2,1)S(1)}, u32[]{:S(2)}, u32[]{:S(2)}) %collective-permute-start.14) | collective-permute-done | bytes 61472 | tf_op jit(solution)/shard_map/ppermute | solution.py:31
  41.3 3.9 %collective-permute-done.16.back_half = bf16[8,3072]{1,0:T(8,128)(2,1)S(1)} collective-permute-done((bf16[8,3072]{1,0:T(8,128)(2,1)S(1)}, bf16[8,3072]{1,0:T(8,128)(2,1)S(1)}, u32[]{:S(2)}, u32[]{:S(2)}) %collective-permute-start.16) | collective-permute-done | bytes 49184 | tf_op jit(solution)/shard_map/ppermute | solution.py:31
  45.2 0.7 %shard_map.70 = bf16[8,3072]{1,0:T(8,128)(2,1)} custom-call(f32[8,128]{1,0:T(8,128)S(1)} %get-tuple-element.16.weights, f32[8,3072]{1,0:T(8,128)S(1)} %get-tuple-element.24.keep, f32[8,3072]{1,0:T(8,128)S(1)} %collective-permute-done.15.got, bf16[8,3072]{1,0:T(8,128)(2,1)S(1)} %collective-permute-done.16.back_half), custom_call_target="tpu_custom_call" | custom-call | tf_op jit(solution)/shard_map/pallas_call | solution.py:249
  (31 shorter events, 2.0 us)
Async XLA Ops:
  0.0 28.6 %collective-permute-start.11 = (bf16[1,256,6144]{2,1,0:T(8,128)(2,1)}, bf16[1,256,6144]{2,1,0:T(8,128)(2,1)S(1)}, u32[]{:S(2)}, u32[]{:S(2)}) collective-permute-start(bf16[1,256,6144]{2,1,0:T(8,128)(2,1)} %down.1), channel_id=1, source_target_pairs={{0,1},{1,0},{2,3},{3,2},{4,5},{5,4},{6,7},{7,6},{8,9},{9,8},{10,11... | collective-permute-start | bytes 9437192 | tf_op jit(solution)/shard_map/ppermute | solution.py:35
  0.5 7.1 %collective-permute-start = (bf16[8,6144]{1,0:T(8,128)(2,1)}, bf16[8,6144]{1,0:T(8,128)(2,1)S(1)}, u32[]{:S(2)}, u32[]{:S(2)}) collective-permute-start(bf16[8,6144]{1,0:T(8,128)(2,1)} %refs_0_.1), channel_id=1, source_target_pairs={{0,4},{1,13},{2,6},{3,15},{4,0},{5,9},{6,2},{7,11},{8,12},{9,5},{1... | collective-permute-start | bytes 294920 | tf_op jit(solution)/shard_map/ppermute | solution.py:31
  3.1 8.4 %collective-permute-start.1 = (bf16[8,6144]{1,0:T(8,128)(2,1)}, bf16[8,6144]{1,0:T(8,128)(2,1)S(1)}, u32[]{:S(2)}, u32[]{:S(2)}) collective-permute-start(bf16[8,6144]{1,0:T(8,128)(2,1)} %refs_0_.1), channel_id=1, source_target_pairs={{0,8},{1,11},{2,10},{3,9},{4,12},{5,15},{6,14},{7,13},{8,0},{9,3},... | collective-permute-start | bytes 294920 | tf_op jit(solution)/shard_map/ppermute | solution.py:31
  5.6 8.3 %collective-permute-start.2 = (bf16[8,6144]{1,0:T(8,128)(2,1)}, bf16[8,6144]{1,0:T(8,128)(2,1)S(1)}, u32[]{:S(2)}, u32[]{:S(2)}) collective-permute-start(bf16[8,6144]{1,0:T(8,128)(2,1)} %refs_0_.1), channel_id=1, source_target_pairs={{0,6},{1,15},{2,4},{3,13},{4,2},{5,11},{6,0},{7,9},{8,14},{9,7},{1... | collective-permute-start | bytes 294920 | tf_op jit(solution)/shard_map/ppermute | solution.py:31
  7.1 8.4 %collective-permute-start.3 = (bf16[8,6144]{1,0:T(8,128)(2,1)}, bf16[8,6144]{1,0:T(8,128)(2,1)S(1)}, u32[]{:S(2)}, u32[]{:S(2)}) collective-permute-start(bf16[8,6144]{1,0:T(8,128)(2,1)} %refs_0_.1), channel_id=1, source_target_pairs={{0,2},{1,3},{2,0},{3,1},{4,6},{5,7},{6,4},{7,5},{8,10},{9,11},{10,... | collective-permute-start | bytes 294920 | tf_op jit(solution)/shard_map/ppermute | solution.py:31
  7.6 7.9 %collective-permute-start.4 = (bf16[8,6144]{1,0:T(8,128)(2,1)S(1)}, bf16[8,6144]{1,0:T(8,128)(2,1)S(1)}, u32[]{:S(2)}, u32[]{:S(2)}) collective-permute-start(bf16[8,6144]{1,0:T(8,128)(2,1)S(1)} %collective-permute-done.refs_1_), channel_id=1, source_target_pairs={{0,1},{1,0},{2,3},{3,2},{4,5},{5,4},{6,7},{7,6},{8,9},{9,8},{10,11... | collective-permute-start | bytes 294920 | tf_op jit(solution)/shard_map/ppermute | solution.py:35
  11.4 4.1 %collective-permute-start.5 = (bf16[8,6144]{1,0:T(8,128)(2,1)S(1)}, bf16[8,6144]{1,0:T(8,128)(2,1)S(1)}, u32[]{:S(2)}, u32[]{:S(2)}) collective-permute-start(bf16[8,6144]{1,0:T(8,128)(2,1)S(1)} %collective-permute-done.1.refs_2_), channel_id=1, source_target_pairs={{0,1},{1,0},{2,3},{3,2},{4,5},{5,4},{6,7},{7,6},{8,9},{9,8},{10,11... | collective-permute-start | bytes 294920 | tf_op jit(solution)/shard_map/ppermute | solution.py:35
  14.0 1.5 %collective-permute-start.6 = (bf16[8,6144]{1,0:T(8,128)(2,1)S(1)}, bf16[8,6144]{1,0:T(8,128)(2,1)S(1)}, u32[]{:S(2)}, u32[]{:S(2)}) collective-permute-start(bf16[8,6144]{1,0:T(8,128)(2,1)S(1)} %collective-permute-done.2.refs_3_), channel_id=1, source_target_pairs={{0,1},{1,0},{2,3},{3,2},{4,5},{5,4},{6,7},{7,6},{8,9},{9,8},{10,11... | collective-permute-start | bytes 294920 | tf_op jit(solution)/shard_map/ppermute | solution.py:35
  15.5 1.9 %copy-start = (bf16[1,6144,256]{2,1,0:T(8,128)(2,1)S(1)}, bf16[1,6144,256]{2,1,0:T(8,128)(2,1)}, u32[]{:S(2)}) copy-start(bf16[1,6144,256]{2,1,0:T(8,128)(2,1)} %refs_8_.1) | copy-start | bytes 9437188
  17.4 1.9 %copy-start.1 = (bf16[1,6144,256]{2,1,0:T(8,128)(2,1)S(1)}, bf16[1,6144,256]{2,1,0:T(8,128)(2,1)}, u32[]{:S(2)}) copy-start(bf16[1,6144,256]{2,1,0:T(8,128)(2,1)} %refs_9_.1) | copy-start | bytes 9437188
  19.3 0.9 %copy-start.3 = (bf16[8,6144]{1,0:T(8,128)(2,1)S(1)}, bf16[8,6144]{1,0:T(8,128)(2,1)}, u32[]{:S(2)}) copy-start(bf16[8,6144]{1,0:T(8,128)(2,1)} %refs_0_.1) | copy-start | bytes 294916
  20.2 1.4 %copy-start.4 = (s32[8,2]{0,1:T(2,128)S(1)}, s32[8,2]{0,1:T(2,128)}, u32[]{:S(2)}) copy-start(s32[8,2]{0,1:T(2,128)} %param.7) | copy-start | bytes 196
  21.4 7.2 %collective-permute-start.7 = (bf16[40,256]{1,0:T(8,128)(2,1)S(1)}, bf16[40,256]{1,0:T(8,128)(2,1)S(1)}, u32[]{:S(2)}, u32[]{:S(2)}) collective-permute-start(bf16[40,256]{1,0:T(8,128)(2,1)S(1)} %get-tuple-element.19), channel_id=1, source_target_pairs={{0,1},{1,0},{2,3},{3,2},{4,5},{5,4},{6,7},{7,6},{8,9},{9,8},{10,11... | collective-permute-start | bytes 61448 | tf_op jit(solution)/shard_map/ppermute | solution.py:35
  21.5 7.1 %copy-start.2 = (bf16[1,256,6144]{2,1,0:T(8,128)(2,1)S(1)}, bf16[1,256,6144]{2,1,0:T(8,128)(2,1)}, u32[]{:S(2)}) copy-start(bf16[1,256,6144]{2,1,0:T(8,128)(2,1)} %down.1) | copy-start | bytes 9437188
  21.7 5.1 %collective-permute-start.10 = (s32[2,8]{1,0:T(2,128)S(1)}, s32[2,8]{1,0:T(2,128)S(1)}, u32[]{:S(2)}, u32[]{:S(2)}) collective-permute-start(s32[2,8]{1,0:T(2,128)S(1)} %shard_map.66), channel_id=1, source_target_pairs={{0,6},{1,15},{2,4},{3,13},{4,2},{5,11},{6,0},{7,9},{8,14},{9,7},{1... | collective-permute-start | bytes 200 | tf_op jit(solution)/shard_map/ppermute | solution.py:31
  23.0 3.8 %collective-permute-start.8 = (s32[2,8]{1,0:T(2,128)S(1)}, s32[2,8]{1,0:T(2,128)S(1)}, u32[]{:S(2)}, u32[]{:S(2)}) collective-permute-start(s32[2,8]{1,0:T(2,128)S(1)} %shard_map.66), channel_id=1, source_target_pairs={{0,4},{1,13},{2,6},{3,15},{4,0},{5,9},{6,2},{7,11},{8,12},{9,5},{1... | collective-permute-start | bytes 200 | tf_op jit(solution)/shard_map/ppermute | solution.py:31
  24.1 4.5 %collective-permute-start.9 = (s32[2,8]{1,0:T(2,128)S(1)}, s32[2,8]{1,0:T(2,128)S(1)}, u32[]{:S(2)}, u32[]{:S(2)}) collective-permute-start(s32[2,8]{1,0:T(2,128)S(1)} %shard_map.66), channel_id=1, source_target_pairs={{0,8},{1,11},{2,10},{3,9},{4,12},{5,15},{6,14},{7,13},{8,0},{9,3},... | collective-permute-start | bytes 200 | tf_op jit(solution)/shard_map/ppermute | solution.py:31
  28.7 6.3 %copy-start.5 = (f32[8,4]{0,1:T(4,128)S(1)}, f32[8,4]{0,1:T(4,128)}, u32[]{:S(2)}) copy-start(f32[8,4]{0,1:T(4,128)} %param.8) | copy-start | bytes 388
  30.0 5.4 %collective-permute-start.12 = (bf16[4,7680]{1,0:T(4,128)(2,1)S(1)}, bf16[4,7680]{1,0:T(4,128)(2,1)S(1)}, u32[]{:S(2)}, u32[]{:S(2)}) collective-permute-start(bf16[4,7680]{1,0:T(4,128)(2,1)S(1)} %get-tuple-element.21), channel_id=1, source_target_pairs={{0,4},{1,13},{2,6},{3,15},{4,0},{5,9},{6,2},{7,11},{8,12},{9,5},{1... | collective-permute-start | bytes 184328 | tf_op jit(solution)/shard_map/ppermute | solution.py:31
  31.0 5.5 %collective-permute-start.13 = (bf16[4,7680]{1,0:T(4,128)(2,1)S(1)}, bf16[4,7680]{1,0:T(4,128)(2,1)S(1)}, u32[]{:S(2)}, u32[]{:S(2)}) collective-permute-start(bf16[4,7680]{1,0:T(4,128)(2,1)S(1)} %get-tuple-element.22), channel_id=1, source_target_pairs={{0,8},{1,11},{2,10},{3,9},{4,12},{5,15},{6,14},{7,13},{8,0},{9,3},... | collective-permute-start | bytes 184328 | tf_op jit(solution)/shard_map/ppermute | solution.py:31
  33.9 6.7 %collective-permute-start.14 = (bf16[4,7680]{1,0:T(4,128)(2,1)S(1)}, bf16[4,7680]{1,0:T(4,128)(2,1)S(1)}, u32[]{:S(2)}, u32[]{:S(2)}) collective-permute-start(bf16[4,7680]{1,0:T(4,128)(2,1)S(1)} %get-tuple-element.23), channel_id=1, source_target_pairs={{0,6},{1,15},{2,4},{3,13},{4,2},{5,11},{6,0},{7,9},{8,14},{9,7},{1... | collective-permute-start | bytes 184328 | tf_op jit(solution)/shard_map/ppermute | solution.py:31
  40.9 4.2 %collective-permute-start.15 = (f32[8,3072]{1,0:T(8,128)S(1)}, f32[8,3072]{1,0:T(8,128)S(1)}, u32[]{:S(2)}, u32[]{:S(2)}) collective-permute-start(f32[8,3072]{1,0:T(8,128)S(1)} %get-tuple-element.25), channel_id=1, source_target_pairs={{0,1},{1,0},{2,3},{3,2},{4,5},{5,4},{6,7},{7,6},{8,9},{9,8},{10,11... | collective-permute-start | bytes 294920 | tf_op jit(solution)/shard_map/ppermute | solution.py:35
  41.0 4.2 %collective-permute-start.16 = (bf16[8,3072]{1,0:T(8,128)(2,1)S(1)}, bf16[8,3072]{1,0:T(8,128)(2,1)S(1)}, u32[]{:S(2)}, u32[]{:S(2)}) collective-permute-start(bf16[8,3072]{1,0:T(8,128)(2,1)S(1)} %get-tuple-element.26), channel_id=1, source_target_pairs={{0,2},{1,3},{2,0},{3,1},{4,6},{5,7},{6,4},{7,5},{8,10},{9,11},{10,... | collective-permute-start | bytes 147464 | tf_op jit(solution)/shard_map/ppermute | solution.py:31

commit v2 on v1

--- a/solution.py
+++ b/solution.py
@@ -18,7 +18,7 @@
 
 def partner_plan(devices):
     if devices == 8:
-        return [(2, 6), (4, 5), (3, 7)], 1
+        return [(2, 7), (4, 5), (3, 6)], 1
     last, *rest = range(1, devices)
     half = len(rest) // 2
     return list(zip(rest[:half], rest[half:])), last
@@ -144,24 +144,34 @@
     give[rows + count * rows :, :] = h[cut - rows : cut]
 
 
-def down_kernel(count, mine, theirs, picks, down, other, *refs):
+def slot_rows(count, rows, hidden, picks, ref):
+    ref[:rows, :] = hidden[:rows, :]
+    for i in range(count):
+        at = slice((i + 1) * rows, (i + 2) * rows)
+        pick = picks[i * rows : (i + 1) * rows, :]
+        ref[at, :] = jnp.dot(pick, hidden[at, :], preferred_element_type=F32).astype(BF16)
+    ref[(count + 1) * rows :, :] = hidden[(count + 1) * rows :, :]
+
+
+def first_kernel(count, mine, picks, down, out, slots):
+    slot_rows(count, picks.shape[1], mine, picks, slots)
+    piece = out.shape[1] // BASE
+    for q in range(BASE):
+        at = slice(q * piece, (q + 1) * piece)
+        out[:, at] = jnp.dot(slots[...], down[0, :, at], preferred_element_type=F32)
+
+
+def down_kernel(count, theirs, picks, begun, other, *refs):
     outs, out_half, own = refs[:count], refs[count], refs[count + 1]
-    left, right, scratch, *spares = refs[count + 2 :]
-    width = down.shape[2]
+    slots, scratch, *spares = refs[count + 2 :]
+    width = begun.shape[1]
     half, piece = width // 2, width // BASE
     rows = own.shape[0]
     here = pl.multiple_of(lax.axis_index("tensor") * half, 128)
-    for hidden, ref in ((mine, left), (theirs, right)):
-        ref[:rows, :] = hidden[:rows, :]
-        for i in range(count):
-            at = slice((i + 1) * rows, (i + 2) * rows)
-            pick = picks[i * rows : (i + 1) * rows, :]
-            ref[at, :] = jnp.dot(pick, hidden[at, :], preferred_element_type=F32).astype(BF16)
-        ref[(count + 1) * rows :, :] = hidden[(count + 1) * rows :, :]
+    slot_rows(count, rows, theirs, picks, slots)
     for q in range(BASE):
         at = slice(q * piece, (q + 1) * piece)
-        y = jnp.dot(left[...], down[0, :, at], preferred_element_type=F32)
-        y += jnp.dot(right[...], other[0, :, at], preferred_element_type=F32)
+        y = begun[:, at] + jnp.dot(slots[...], other[0, :, at], preferred_element_type=F32)
         scratch[:rows, at] = y[:rows]
         scratch[rows:, at] = y[(count + 1) * rows :]
         for i in range(count):
@@ -231,11 +241,15 @@
     got = swap_cores(give)
     slots = S((BASE, width * CAP // BASE), bf16)
     spare, spread = pltpu.VMEM((BASE, width // BASE), f32), pltpu.VMEM((rows, width), f32)
+    begun = call(
+        functools.partial(first_kernel, count), 3, S((cut, width), f32), 8 * MIB,
+        [pltpu.VMEM((cut, hidden), bf16)],
+    )(keep, picks, down)
     *outs, out_half, own = call(
-        functools.partial(down_kernel, count), 5,
+        functools.partial(down_kernel, count), 4,
         [slots] * count + [S((rows, half), bf16), S((rows, half), f32)], 14 * MIB,
-        [pltpu.VMEM((cut, hidden), bf16)] * 2 + [pltpu.VMEM((2 * rows, width), f32)] + [spare] * count,
-    )(keep, got, picks, down, other)
+        [pltpu.VMEM((cut, hidden), bf16), pltpu.VMEM((2 * rows, width), f32)] + [spare] * count,
+    )(got, picks, begun, other)
     back = []
     for o, offsets in zip([*outs, out_half], [*plan, (last, last)]):
         back.append(exchange(o, devices, offsets))

time: 46.1 us -> 46.2 us (level)
  starting transfers between devices: 21.9 us -> 20.9 us
  waiting for transfers between devices: 15.1 us -> 16 us
    ppermute x6, starting transfers between devices: 4.5 us -> 3.25 us  [swap_cores(): return lax.ppermute(x, 'tensor', [(0, 1), (1, 0)])]
    ppermute x6, waiting for transfers between devices: 0.02 us -> 0.75 us  [swap_cores(): return lax.ppermute(x, 'tensor', [(0, 1), (1, 0)])]
    pallas_call x1 -> x2, Pallas kernels: 1.3 us -> 1.51 us  [the longest x1 0.76 us: layer(): call(functools.partial(down_kernel, count), 4, [slots] * count + [S((rows...]
  transfers between devices with their start and end apart: 17 -> 17, of which waited for: 6 -> 8; matrix products, arithmetic and copies ran while one was open for 0% -> 0% of each run, Pallas kernels for 4% -> 5%
where the time goes in v2:
time: 46.2 us; the launch traced here: 46 us
  starting transfers between devices  20.9 us (45%)
  waiting for transfers between devices  16 us (35%)
  local copies, waits for them, and re-layouts  4.85 us (10%)
  Pallas kernels  4.15 us (9%)
    ppermute x11, starting transfers between devices, exchange(): return lax.ppermute(x, AXES, pairs)  17.7 us
    ppermute x11, waiting for transfers between devices, exchange(): return lax.ppermute(x, AXES, pairs)  15.2 us
    unnamed x14, local copies, waits for them, and re-layouts  4.85 us
    ppermute x6, starting transfers between devices, swap_cores(): return lax.ppermute(x, 'tensor', [(0, 1), (1, 0)])  3.25 us
    pallas_call x1, Pallas kernels, layer(): call(functools.partial(hidden_kernel, count), 2 * count + 4, [S((cut, hid...  1.21 us
  transfers between devices with their start and end apart: 17, of which 8 were waited for; matrix products, arithmetic and copies ran while one was open for 0% of the time, Pallas kernels for 5%

profile of v2, /device:TPU:0, one launch (start us, length us, event | category | flops | bytes accessed | tf_op | source)
XLA Modules:
  0.0 46.0 jit_solution(3735259013371514533)
XLA Ops:
  0.5 2.6 %collective-permute-start = (bf16[8,6144]{1,0:T(8,128)(2,1)}, bf16[8,6144]{1,0:T(8,128)(2,1)S(1)}, u32[]{:S(2)}, u32[]{:S(2)}) collective-permute-start(bf16[8,6144]{1,0:T(8,128)(2,1)} %refs_0_.1), channel_id=1, source_target_pairs={{0,4},{1,15},{2,6},{3,13},{4,0},{5,11},{6,2},{7,9},{8,12},{9,7},{1... | collective-permute-start | bytes 294920 | tf_op jit(solution)/shard_map/ppermute | solution.py:31
  3.1 2.6 %collective-permute-start.1 = (bf16[8,6144]{1,0:T(8,128)(2,1)}, bf16[8,6144]{1,0:T(8,128)(2,1)S(1)}, u32[]{:S(2)}, u32[]{:S(2)}) collective-permute-start(bf16[8,6144]{1,0:T(8,128)(2,1)} %refs_0_.1), channel_id=1, source_target_pairs={{0,8},{1,11},{2,10},{3,9},{4,12},{5,15},{6,14},{7,13},{8,0},{9,3},... | collective-permute-start | bytes 294920 | tf_op jit(solution)/shard_map/ppermute | solution.py:31
  5.6 1.4 %collective-permute-start.2 = (bf16[8,6144]{1,0:T(8,128)(2,1)}, bf16[8,6144]{1,0:T(8,128)(2,1)S(1)}, u32[]{:S(2)}, u32[]{:S(2)}) collective-permute-start(bf16[8,6144]{1,0:T(8,128)(2,1)} %refs_0_.1), channel_id=1, source_target_pairs={{0,6},{1,13},{2,4},{3,15},{4,2},{5,9},{6,0},{7,11},{8,14},{9,5},{1... | collective-permute-start | bytes 294920 | tf_op jit(solution)/shard_map/ppermute | solution.py:31
  7.6 1.6 %collective-permute-start.4 = (bf16[8,6144]{1,0:T(8,128)(2,1)S(1)}, bf16[8,6144]{1,0:T(8,128)(2,1)S(1)}, u32[]{:S(2)}, u32[]{:S(2)}) collective-permute-start(bf16[8,6144]{1,0:T(8,128)(2,1)S(1)} %collective-permute-done.refs_1_), channel_id=1, source_target_pairs={{0,1},{1,0},{2,3},{3,2},{4,5},{5,4},{6,7},{7,6},{8,9},{9,8},{10,11... | collective-permute-start | bytes 294920 | tf_op jit(solution)/shard_map/ppermute | solution.py:35
  9.2 3.9 %collective-permute-done.1.refs_2_ = bf16[8,6144]{1,0:T(8,128)(2,1)S(1)} collective-permute-done((bf16[8,6144]{1,0:T(8,128)(2,1)}, bf16[8,6144]{1,0:T(8,128)(2,1)S(1)}, u32[]{:S(2)}, u32[]{:S(2)}) %collective-permute-start.1) | collective-permute-done | bytes 98336 | tf_op jit(solution)/shard_map/ppermute | solution.py:31
  13.1 0.9 %collective-permute-start.5 = (bf16[8,6144]{1,0:T(8,128)(2,1)S(1)}, bf16[8,6144]{1,0:T(8,128)(2,1)S(1)}, u32[]{:S(2)}, u32[]{:S(2)}) collective-permute-start(bf16[8,6144]{1,0:T(8,128)(2,1)S(1)} %collective-permute-done.1.refs_2_), channel_id=1, source_target_pairs={{0,1},{1,0},{2,3},{3,2},{4,5},{5,4},{6,7},{7,6},{8,9},{9,8},{10,11... | collective-permute-start | bytes 294920 | tf_op jit(solution)/shard_map/ppermute | solution.py:35
  15.3 1.9 %copy-done = bf16[1,6144,256]{2,1,0:T(8,128)(2,1)S(1)} copy-done((bf16[1,6144,256]{2,1,0:T(8,128)(2,1)S(1)}, bf16[1,6144,256]{2,1,0:T(8,128)(2,1)}, u32[]{:S(2)}) %copy-start) | copy-done | bytes 3145752
  17.2 1.9 %copy-done.1 = bf16[1,6144,256]{2,1,0:T(8,128)(2,1)S(1)} copy-done((bf16[1,6144,256]{2,1,0:T(8,128)(2,1)S(1)}, bf16[1,6144,256]{2,1,0:T(8,128)(2,1)}, u32[]{:S(2)}) %copy-start.1) | copy-done | bytes 3145752
  19.1 0.9 %copy-done.3 = bf16[8,6144]{1,0:T(8,128)(2,1)S(1)} copy-done((bf16[8,6144]{1,0:T(8,128)(2,1)S(1)}, bf16[8,6144]{1,0:T(8,128)(2,1)}, u32[]{:S(2)}) %copy-start.3) | copy-done | bytes 98328
  20.0 1.2 %shard_map.65 = (bf16[40,256]{1,0:T(8,128)(2,1)S(1)}, bf16[40,256]{1,0:T(8,128)(2,1)S(1)}) custom-call(bf16[8,6144]{1,0:T(8,128)(2,1)S(1)} %copy-done.3, bf16[8,6144]{1,0:T(8,128)(2,1)S(1)} %collective-permute-done.refs_1_, bf16[8,6144]{1,0:T(8,128)(2,1)S(1)} %collective-permute-done.1.refs_2_, bf16[8,6144]{1,0:T(8,128)(2,1)S(1)} %collective-permute-done.2.refs_3_, ...), custom_call_target="tpu_custom_call" | custom-call | tf_op jit(solution)/shard_map/pallas_call | solution.py:237
  21.5 1.8 %collective-permute-start.10 = (s32[2,8]{1,0:T(2,128)S(1)}, s32[2,8]{1,0:T(2,128)S(1)}, u32[]{:S(2)}, u32[]{:S(2)}) collective-permute-start(s32[2,8]{1,0:T(2,128)S(1)} %shard_map.66), channel_id=1, source_target_pairs={{0,6},{1,13},{2,4},{3,15},{4,2},{5,9},{6,0},{7,11},{8,14},{9,5},{1... | collective-permute-start | bytes 200 | tf_op jit(solution)/shard_map/ppermute | solution.py:31
  23.3 1.1 %collective-permute-start.8 = (s32[2,8]{1,0:T(2,128)S(1)}, s32[2,8]{1,0:T(2,128)S(1)}, u32[]{:S(2)}, u32[]{:S(2)}) collective-permute-start(s32[2,8]{1,0:T(2,128)S(1)} %shard_map.66), channel_id=1, source_target_pairs={{0,4},{1,15},{2,6},{3,13},{4,0},{5,11},{6,2},{7,9},{8,12},{9,7},{1... | collective-permute-start | bytes 200 | tf_op jit(solution)/shard_map/ppermute | solution.py:31
  24.4 2.4 %collective-permute-start.9 = (s32[2,8]{1,0:T(2,128)S(1)}, s32[2,8]{1,0:T(2,128)S(1)}, u32[]{:S(2)}, u32[]{:S(2)}) collective-permute-start(s32[2,8]{1,0:T(2,128)S(1)} %shard_map.66), channel_id=1, source_target_pairs={{0,8},{1,11},{2,10},{3,9},{4,12},{5,15},{6,14},{7,13},{8,0},{9,3},... | collective-permute-start | bytes 200 | tf_op jit(solution)/shard_map/ppermute | solution.py:31
  26.9 2.0 %collective-permute-done.9.refs_1_ = s32[2,8]{1,0:T(2,128)S(1)} collective-permute-done((s32[2,8]{1,0:T(2,128)S(1)}, s32[2,8]{1,0:T(2,128)S(1)}, u32[]{:S(2)}, u32[]{:S(2)}) %collective-permute-start.9) | collective-permute-done | bytes 96 | tf_op jit(solution)/shard_map/ppermute | solution.py:31
  28.9 0.7 %shard_map.68.begun = f32[40,6144]{1,0:T(8,128)S(1)} custom-call(bf16[40,256]{1,0:T(8,128)(2,1)S(1)} %get-tuple-element.19.mine, bf16[24,8]{1,0:T(8,128)(2,1)S(1)} %shard_map.67.picks, bf16[1,256,6144]{2,1,0:T(8,128)(2,1)S(1)} %copy-done.2), custom_call_target="tpu_custom_call" | custom-call | tf_op jit(solution)/shard_map/pallas_call | solution.py:244
  29.7 0.8 %shard_map.69 = (bf16[4,7680]{1,0:T(4,128)(2,1)S(1)}, bf16[4,7680]{1,0:T(4,128)(2,1)S(1)}, bf16[4,7680]{1,0:T(4,128)(2,1)S(1)}, bf16[8,3072]{1,0:T(8,128)(2,1)S(1)}, f32[8,3072]{1,0:T(8,128)S(1)}) custom-call(bf16[40,256]{1,0:T(8,128)(2,1)S(1)} %collective-permute-done.7.theirs, bf16[24,8]{1,0:T(8,128)(2,1)S(1)} %shard_map.67.picks, ...), custom_call_target="tpu_custom_call" | custom-call | tf_op jit(solution)/shard_map/pallas_call | solution.py:248
  30.5 1.0 %collective-permute-start.12 = (bf16[4,7680]{1,0:T(4,128)(2,1)S(1)}, bf16[4,7680]{1,0:T(4,128)(2,1)S(1)}, u32[]{:S(2)}, u32[]{:S(2)}) collective-permute-start(bf16[4,7680]{1,0:T(4,128)(2,1)S(1)} %get-tuple-element.21), channel_id=1, source_target_pairs={{0,4},{1,15},{2,6},{3,13},{4,0},{5,11},{6,2},{7,9},{8,12},{9,7},{1... | collective-permute-start | bytes 184328 | tf_op jit(solution)/shard_map/ppermute | solution.py:31
  31.4 2.7 %collective-permute-start.13 = (bf16[4,7680]{1,0:T(4,128)(2,1)S(1)}, bf16[4,7680]{1,0:T(4,128)(2,1)S(1)}, u32[]{:S(2)}, u32[]{:S(2)}) collective-permute-start(bf16[4,7680]{1,0:T(4,128)(2,1)S(1)} %get-tuple-element.22), channel_id=1, source_target_pairs={{0,8},{1,11},{2,10},{3,9},{4,12},{5,15},{6,14},{7,13},{8,0},{9,3},... | collective-permute-start | bytes 184328 | tf_op jit(solution)/shard_map/ppermute | solution.py:31
  34.1 0.9 %collective-permute-start.14 = (bf16[4,7680]{1,0:T(4,128)(2,1)S(1)}, bf16[4,7680]{1,0:T(4,128)(2,1)S(1)}, u32[]{:S(2)}, u32[]{:S(2)}) collective-permute-start(bf16[4,7680]{1,0:T(4,128)(2,1)S(1)} %get-tuple-element.23), channel_id=1, source_target_pairs={{0,6},{1,13},{2,4},{3,15},{4,2},{5,9},{6,0},{7,11},{8,14},{9,5},{1... | collective-permute-start | bytes 184328 | tf_op jit(solution)/shard_map/ppermute | solution.py:31
  35.6 1.1 %collective-permute-done.13.refs_1_ = bf16[4,7680]{1,0:T(4,128)(2,1)S(1)} collective-permute-done((bf16[4,7680]{1,0:T(4,128)(2,1)S(1)}, bf16[4,7680]{1,0:T(4,128)(2,1)S(1)}, u32[]{:S(2)}, u32[]{:S(2)}) %collective-permute-start.13) | collective-permute-done | bytes 61472 | tf_op jit(solution)/shard_map/ppermute | solution.py:31
  36.7 4.1 %collective-permute-done.14.refs_2_ = bf16[4,7680]{1,0:T(4,128)(2,1)S(1)} collective-permute-done((bf16[4,7680]{1,0:T(4,128)(2,1)S(1)}, bf16[4,7680]{1,0:T(4,128)(2,1)S(1)}, u32[]{:S(2)}, u32[]{:S(2)}) %collective-permute-start.14) | collective-permute-done | bytes 61472 | tf_op jit(solution)/shard_map/ppermute | solution.py:31
  41.2 0.7 %collective-permute-start.16 = (bf16[8,3072]{1,0:T(8,128)(2,1)S(1)}, bf16[8,3072]{1,0:T(8,128)(2,1)S(1)}, u32[]{:S(2)}, u32[]{:S(2)}) collective-permute-start(bf16[8,3072]{1,0:T(8,128)(2,1)S(1)} %get-tuple-element.26), channel_id=1, source_target_pairs={{0,2},{1,3},{2,0},{3,1},{4,6},{5,7},{6,4},{7,5},{8,10},{9,11},{10,... | collective-permute-start | bytes 147464 | tf_op jit(solution)/shard_map/ppermute | solution.py:31
  41.9 3.4 %collective-permute-done.16.back_half = bf16[8,3072]{1,0:T(8,128)(2,1)S(1)} collective-permute-done((bf16[8,3072]{1,0:T(8,128)(2,1)S(1)}, bf16[8,3072]{1,0:T(8,128)(2,1)S(1)}, u32[]{:S(2)}, u32[]{:S(2)}) %collective-permute-start.16) | collective-permute-done | bytes 49184 | tf_op jit(solution)/shard_map/ppermute | solution.py:31
  45.3 0.7 %shard_map.71 = bf16[8,3072]{1,0:T(8,128)(2,1)} custom-call(f32[8,128]{1,0:T(8,128)S(1)} %get-tuple-element.16.weights, f32[8,3072]{1,0:T(8,128)S(1)} %get-tuple-element.24.keep, f32[8,3072]{1,0:T(8,128)S(1)} %collective-permute-done.15.got, bf16[8,3072]{1,0:T(8,128)(2,1)S(1)} %collective-permute-done.16.back_half), custom_call_target="tpu_custom_call" | custom-call | tf_op jit(solution)/shard_map/pallas_call | solution.py:263
  (32 shorter events, 3.6 us)
Async XLA Ops:
  0.0 29.7 %collective-permute-start.11 = (bf16[1,256,6144]{2,1,0:T(8,128)(2,1)}, bf16[1,256,6144]{2,1,0:T(8,128)(2,1)S(1)}, u32[]{:S(2)}, u32[]{:S(2)}) collective-permute-start(bf16[1,256,6144]{2,1,0:T(8,128)(2,1)} %down.1), channel_id=1, source_target_pairs={{0,1},{1,0},{2,3},{3,2},{4,5},{5,4},{6,7},{7,6},{8,9},{9,8},{10,11... | collective-permute-start | bytes 9437192 | tf_op jit(solution)/shard_map/ppermute | solution.py:35
  0.5 7.1 %collective-permute-start = (bf16[8,6144]{1,0:T(8,128)(2,1)}, bf16[8,6144]{1,0:T(8,128)(2,1)S(1)}, u32[]{:S(2)}, u32[]{:S(2)}) collective-permute-start(bf16[8,6144]{1,0:T(8,128)(2,1)} %refs_0_.1), channel_id=1, source_target_pairs={{0,4},{1,15},{2,6},{3,13},{4,0},{5,11},{6,2},{7,9},{8,12},{9,7},{1... | collective-permute-start | bytes 294920 | tf_op jit(solution)/shard_map/ppermute | solution.py:31
  3.1 10.1 %collective-permute-start.1 = (bf16[8,6144]{1,0:T(8,128)(2,1)}, bf16[8,6144]{1,0:T(8,128)(2,1)S(1)}, u32[]{:S(2)}, u32[]{:S(2)}) collective-permute-start(bf16[8,6144]{1,0:T(8,128)(2,1)} %refs_0_.1), channel_id=1, source_target_pairs={{0,8},{1,11},{2,10},{3,9},{4,12},{5,15},{6,14},{7,13},{8,0},{9,3},... | collective-permute-start | bytes 294920 | tf_op jit(solution)/shard_map/ppermute | solution.py:31
  5.6 8.3 %collective-permute-start.2 = (bf16[8,6144]{1,0:T(8,128)(2,1)}, bf16[8,6144]{1,0:T(8,128)(2,1)S(1)}, u32[]{:S(2)}, u32[]{:S(2)}) collective-permute-start(bf16[8,6144]{1,0:T(8,128)(2,1)} %refs_0_.1), channel_id=1, source_target_pairs={{0,6},{1,13},{2,4},{3,15},{4,2},{5,9},{6,0},{7,11},{8,14},{9,5},{1... | collective-permute-start | bytes 294920 | tf_op jit(solution)/shard_map/ppermute | solution.py:31
  7.1 7.5 %collective-permute-start.3 = (bf16[8,6144]{1,0:T(8,128)(2,1)}, bf16[8,6144]{1,0:T(8,128)(2,1)S(1)}, u32[]{:S(2)}, u32[]{:S(2)}) collective-permute-start(bf16[8,6144]{1,0:T(8,128)(2,1)} %refs_0_.1), channel_id=1, source_target_pairs={{0,2},{1,3},{2,0},{3,1},{4,6},{5,7},{6,4},{7,5},{8,10},{9,11},{10,... | collective-permute-start | bytes 294920 | tf_op jit(solution)/shard_map/ppermute | solution.py:31
  7.6 7.0 %collective-permute-start.4 = (bf16[8,6144]{1,0:T(8,128)(2,1)S(1)}, bf16[8,6144]{1,0:T(8,128)(2,1)S(1)}, u32[]{:S(2)}, u32[]{:S(2)}) collective-permute-start(bf16[8,6144]{1,0:T(8,128)(2,1)S(1)} %collective-permute-done.refs_1_), channel_id=1, source_target_pairs={{0,1},{1,0},{2,3},{3,2},{4,5},{5,4},{6,7},{7,6},{8,9},{9,8},{10,11... | collective-permute-start | bytes 294920 | tf_op jit(solution)/shard_map/ppermute | solution.py:35
  13.1 1.8 %collective-permute-start.5 = (bf16[8,6144]{1,0:T(8,128)(2,1)S(1)}, bf16[8,6144]{1,0:T(8,128)(2,1)S(1)}, u32[]{:S(2)}, u32[]{:S(2)}) collective-permute-start(bf16[8,6144]{1,0:T(8,128)(2,1)S(1)} %collective-permute-done.1.refs_2_), channel_id=1, source_target_pairs={{0,1},{1,0},{2,3},{3,2},{4,5},{5,4},{6,7},{7,6},{8,9},{9,8},{10,11... | collective-permute-start | bytes 294920 | tf_op jit(solution)/shard_map/ppermute | solution.py:35
  14.0 1.3 %collective-permute-start.6 = (bf16[8,6144]{1,0:T(8,128)(2,1)S(1)}, bf16[8,6144]{1,0:T(8,128)(2,1)S(1)}, u32[]{:S(2)}, u32[]{:S(2)}) collective-permute-start(bf16[8,6144]{1,0:T(8,128)(2,1)S(1)} %collective-permute-done.2.refs_3_), channel_id=1, source_target_pairs={{0,1},{1,0},{2,3},{3,2},{4,5},{5,4},{6,7},{7,6},{8,9},{9,8},{10,11... | collective-permute-start | bytes 294920 | tf_op jit(solution)/shard_map/ppermute | solution.py:35
  15.3 1.9 %copy-start = (bf16[1,6144,256]{2,1,0:T(8,128)(2,1)S(1)}, bf16[1,6144,256]{2,1,0:T(8,128)(2,1)}, u32[]{:S(2)}) copy-start(bf16[1,6144,256]{2,1,0:T(8,128)(2,1)} %refs_8_.1) | copy-start | bytes 9437188
  17.2 1.9 %copy-start.1 = (bf16[1,6144,256]{2,1,0:T(8,128)(2,1)S(1)}, bf16[1,6144,256]{2,1,0:T(8,128)(2,1)}, u32[]{:S(2)}) copy-start(bf16[1,6144,256]{2,1,0:T(8,128)(2,1)} %refs_9_.1) | copy-start | bytes 9437188
  19.1 0.9 %copy-start.3 = (bf16[8,6144]{1,0:T(8,128)(2,1)S(1)}, bf16[8,6144]{1,0:T(8,128)(2,1)}, u32[]{:S(2)}) copy-start(bf16[8,6144]{1,0:T(8,128)(2,1)} %refs_0_.1) | copy-start | bytes 294916
  20.0 1.4 %copy-start.4 = (s32[8,2]{0,1:T(2,128)S(1)}, s32[8,2]{0,1:T(2,128)}, u32[]{:S(2)}) copy-start(s32[8,2]{0,1:T(2,128)} %param.7) | copy-start | bytes 196
  21.2 8.5 %collective-permute-start.7 = (bf16[40,256]{1,0:T(8,128)(2,1)S(1)}, bf16[40,256]{1,0:T(8,128)(2,1)S(1)}, u32[]{:S(2)}, u32[]{:S(2)}) collective-permute-start(bf16[40,256]{1,0:T(8,128)(2,1)S(1)} %get-tuple-element.18), channel_id=1, source_target_pairs={{0,1},{1,0},{2,3},{3,2},{4,5},{5,4},{6,7},{7,6},{8,9},{9,8},{10,11... | collective-permute-start | bytes 61448 | tf_op jit(solution)/shard_map/ppermute | solution.py:35
  21.4 7.5 %copy-start.2 = (bf16[1,256,6144]{2,1,0:T(8,128)(2,1)S(1)}, bf16[1,256,6144]{2,1,0:T(8,128)(2,1)}, u32[]{:S(2)}) copy-start(bf16[1,256,6144]{2,1,0:T(8,128)(2,1)} %down.1) | copy-start | bytes 9437188
  21.5 5.3 %collective-permute-start.10 = (s32[2,8]{1,0:T(2,128)S(1)}, s32[2,8]{1,0:T(2,128)S(1)}, u32[]{:S(2)}, u32[]{:S(2)}) collective-permute-start(s32[2,8]{1,0:T(2,128)S(1)} %shard_map.66), channel_id=1, source_target_pairs={{0,6},{1,13},{2,4},{3,15},{4,2},{5,9},{6,0},{7,11},{8,14},{9,5},{1... | collective-permute-start | bytes 200 | tf_op jit(solution)/shard_map/ppermute | solution.py:31
  23.3 3.6 %collective-permute-start.8 = (s32[2,8]{1,0:T(2,128)S(1)}, s32[2,8]{1,0:T(2,128)S(1)}, u32[]{:S(2)}, u32[]{:S(2)}) collective-permute-start(s32[2,8]{1,0:T(2,128)S(1)} %shard_map.66), channel_id=1, source_target_pairs={{0,4},{1,15},{2,6},{3,13},{4,0},{5,11},{6,2},{7,9},{8,12},{9,7},{1... | collective-permute-start | bytes 200 | tf_op jit(solution)/shard_map/ppermute | solution.py:31
  24.4 4.5 %collective-permute-start.9 = (s32[2,8]{1,0:T(2,128)S(1)}, s32[2,8]{1,0:T(2,128)S(1)}, u32[]{:S(2)}, u32[]{:S(2)}) collective-permute-start(s32[2,8]{1,0:T(2,128)S(1)} %shard_map.66), channel_id=1, source_target_pairs={{0,8},{1,11},{2,10},{3,9},{4,12},{5,15},{6,14},{7,13},{8,0},{9,3},... | collective-permute-start | bytes 200 | tf_op jit(solution)/shard_map/ppermute | solution.py:31
  28.9 6.2 %copy-start.5 = (f32[8,4]{0,1:T(4,128)S(1)}, f32[8,4]{0,1:T(4,128)}, u32[]{:S(2)}) copy-start(f32[8,4]{0,1:T(4,128)} %param.8) | copy-start | bytes 388
  30.5 5.1 %collective-permute-start.12 = (bf16[4,7680]{1,0:T(4,128)(2,1)S(1)}, bf16[4,7680]{1,0:T(4,128)(2,1)S(1)}, u32[]{:S(2)}, u32[]{:S(2)}) collective-permute-start(bf16[4,7680]{1,0:T(4,128)(2,1)S(1)} %get-tuple-element.21), channel_id=1, source_target_pairs={{0,4},{1,15},{2,6},{3,13},{4,0},{5,11},{6,2},{7,9},{8,12},{9,7},{1... | collective-permute-start | bytes 184328 | tf_op jit(solution)/shard_map/ppermute | solution.py:31
  31.4 5.2 %collective-permute-start.13 = (bf16[4,7680]{1,0:T(4,128)(2,1)S(1)}, bf16[4,7680]{1,0:T(4,128)(2,1)S(1)}, u32[]{:S(2)}, u32[]{:S(2)}) collective-permute-start(bf16[4,7680]{1,0:T(4,128)(2,1)S(1)} %get-tuple-element.22), channel_id=1, source_target_pairs={{0,8},{1,11},{2,10},{3,9},{4,12},{5,15},{6,14},{7,13},{8,0},{9,3},... | collective-permute-start | bytes 184328 | tf_op jit(solution)/shard_map/ppermute | solution.py:31
  34.1 6.7 %collective-permute-start.14 = (bf16[4,7680]{1,0:T(4,128)(2,1)S(1)}, bf16[4,7680]{1,0:T(4,128)(2,1)S(1)}, u32[]{:S(2)}, u32[]{:S(2)}) collective-permute-start(bf16[4,7680]{1,0:T(4,128)(2,1)S(1)} %get-tuple-element.23), channel_id=1, source_target_pairs={{0,6},{1,13},{2,4},{3,15},{4,2},{5,9},{6,0},{7,11},{8,14},{9,5},{1... | collective-permute-start | bytes 184328 | tf_op jit(solution)/shard_map/ppermute | solution.py:31
  41.1 4.2 %collective-permute-start.15 = (f32[8,3072]{1,0:T(8,128)S(1)}, f32[8,3072]{1,0:T(8,128)S(1)}, u32[]{:S(2)}, u32[]{:S(2)}) collective-permute-start(f32[8,3072]{1,0:T(8,128)S(1)} %get-tuple-element.25), channel_id=1, source_target_pairs={{0,1},{1,0},{2,3},{3,2},{4,5},{5,4},{6,7},{7,6},{8,9},{9,8},{10,11... | collective-permute-start | bytes 294920 | tf_op jit(solution)/shard_map/ppermute | solution.py:35
  41.2 4.2 %collective-permute-start.16 = (bf16[8,3072]{1,0:T(8,128)(2,1)S(1)}, bf16[8,3072]{1,0:T(8,128)(2,1)S(1)}, u32[]{:S(2)}, u32[]{:S(2)}) collective-permute-start(bf16[8,3072]{1,0:T(8,128)(2,1)S(1)} %get-tuple-element.26), channel_id=1, source_target_pairs={{0,2},{1,3},{2,0},{3,1},{4,6},{5,7},{6,4},{7,5},{8,10},{9,11},{10,... | collective-permute-start | bytes 147464 | tf_op jit(solution)/shard_map/ppermute | solution.py:31

commit v3 on v2

--- a/solution.py
+++ b/solution.py
@@ -18,10 +18,10 @@
 
 def partner_plan(devices):
     if devices == 8:
-        return [(2, 7), (4, 5), (3, 6)], 1
+        return [(2, 6), (5, 4), (3, 7)], 1, 1
     last, *rest = range(1, devices)
     half = len(rest) // 2
-    return list(zip(rest[:half], rest[half:])), last
+    return list(zip(rest[:half], rest[half:])), half // 3, last
 
 
 def exchange(x, devices, offsets):
@@ -61,6 +61,39 @@
     for q in range(BASE):
         scratch[BASE:CAP, q * piece : (q + 1) * piece] = beside[q : q + 1]
     return scratch[...].astype(BF16)
+
+
+def pack(rows, first, width, ref, spare):
+    piece = width // BASE
+    ref[:, first : first + rows.shape[1]] = rows[:BASE].astype(BF16)
+    for q in range(BASE):
+        at = q * piece - first
+        if 0 <= at < rows.shape[1]:
+            spare[q : q + 1, :] = rows[BASE:CAP, at : at + piece]
+
+
+def earlier_kernel(out):
+    row, column = (lax.broadcasted_iota(jnp.int32, out.shape, d) for d in range(2))
+    out[...] = jnp.where(row < column, 1.0, 0.0).astype(BF16)
+
+
+def pack_kernel(packed, segments, tokens, routes, before, *refs):
+    outs, spare = refs[:-1], refs[-1]
+    rows, width = tokens.shape
+    shape = (len(packed) * rows, rows)
+    row = lax.broadcasted_iota(jnp.int32, shape, 0)
+    expert = jnp.zeros(shape, jnp.int32)
+    for i, offsets in enumerate(packed):
+        expert = jnp.where(row // rows == i, expert_at(offsets, segments), expert)
+    named = (routes[0:1, :] == expert) | (routes[1:2, :] == expert)
+    slot = jnp.dot(
+        jnp.where(named, 1.0, 0.0).astype(BF16), before[...], preferred_element_type=F32
+    )
+    pick = jnp.where(named & (slot == (row % rows).astype(F32)), 1.0, 0.0).astype(BF16)
+    picked = jnp.dot(pick, tokens[...], preferred_element_type=F32)
+    for i, out in enumerate(outs):
+        pack(picked[i * rows : (i + 1) * rows], 0, width, out, spare)
+        out[:, width:] = spare[...].astype(BF16)
 
 
 def number_kernel(experts, routes, out):
@@ -130,10 +163,12 @@
 
 
 def hidden_kernel(count, *refs):
-    blocks, (gate, up, keep, give, x) = refs[:-5], refs[-5:]
+    total = 2 * count + 2
+    blocks, (gate, up, keep, give, x), spreads = refs[:total], refs[total : total + 5], list(refs[total + 5 :])
     rows, _ = blocks[0].shape
     for i, block in enumerate(blocks):
-        x[i * rows : (i + 1) * rows, :] = block[...]
+        packed = block.shape[0] != rows
+        x[i * rows : (i + 1) * rows, :] = unpack(block, spreads.pop()) if packed else block[...]
     g = jnp.dot(x[...], gate[0], preferred_element_type=jnp.float32)
     u = jnp.dot(x[...], up[0], preferred_element_type=jnp.float32)
     h = (g / (1.0 + jnp.exp(-g)) * u).astype(jnp.bfloat16)
@@ -144,17 +179,19 @@
     give[rows + count * rows :, :] = h[cut - rows : cut]
 
 
-def slot_rows(count, rows, hidden, picks, ref):
+def slot_rows(hidden, picks, ref):
+    rows = picks.shape[1]
+    whole = picks.shape[0] // rows
     ref[:rows, :] = hidden[:rows, :]
-    for i in range(count):
+    for i in range(whole):
         at = slice((i + 1) * rows, (i + 2) * rows)
         pick = picks[i * rows : (i + 1) * rows, :]
         ref[at, :] = jnp.dot(pick, hidden[at, :], preferred_element_type=F32).astype(BF16)
-    ref[(count + 1) * rows :, :] = hidden[(count + 1) * rows :, :]
-
-
-def first_kernel(count, mine, picks, down, out, slots):
-    slot_rows(count, picks.shape[1], mine, picks, slots)
+    ref[(whole + 1) * rows :, :] = hidden[(whole + 1) * rows :, :]
+
+
+def first_kernel(mine, picks, down, out, slots):
+    slot_rows(mine, picks, slots)
     piece = out.shape[1] // BASE
     for q in range(BASE):
         at = slice(q * piece, (q + 1) * piece)
@@ -168,7 +205,7 @@
     half, piece = width // 2, width // BASE
     rows = own.shape[0]
     here = pl.multiple_of(lax.axis_index("tensor") * half, 128)
-    slot_rows(count, rows, theirs, picks, slots)
+    slot_rows(theirs, picks, slots)
     for q in range(BASE):
         at = slice(q * piece, (q + 1) * piece)
         y = begun[:, at] + jnp.dot(slots[...], other[0, :, at], preferred_element_type=F32)
@@ -208,14 +245,23 @@
     rows, width = tokens.shape
     devices = lax.axis_size("expert")
     segments = devices // logits.shape[1]
-    plan, last = partner_plan(devices)
+    plan, whole, last = partner_plan(devices)
     count = len(plan)
     half, hidden = width // 2, gate.shape[2]
     bf16, f32 = jnp.bfloat16, jnp.float32
     S = jax.ShapeDtypeStruct
+    slots = S((BASE, width * CAP // BASE), bf16)
+    spare, spread = pltpu.VMEM((BASE, width // BASE), f32), pltpu.VMEM((rows, width), f32)
+    hint = pl.CostEstimate(flops=4_000_000_000, bytes_accessed=20 * MIB, transcendentals=0)
+    before = call(earlier_kernel, 0, S((rows, rows), bf16), 1 * MIB, cost=hint)()
+    packed = call(
+        functools.partial(pack_kernel, plan[whole:], segments), 3, [slots] * (count - whole),
+        2 * MIB + count * MIB // 4, [spare],
+    )(tokens, routes.T, before)
     mine = []
-    for offsets in [*plan, (last, last)]:
-        mine.append(exchange(tokens, devices, offsets))
+    for j, offsets in enumerate([*plan, (last, last)]):
+        x = packed[j - whole] if whole <= j < count else tokens
+        mine.append(exchange(x, devices, offsets))
     mine, near = mine[:-1], mine[-1]
     other = swap_cores(down)
     hint = pl.CostEstimate(flops=4_000_000_000, bytes_accessed=20 * MIB, transcendentals=0)
@@ -223,26 +269,25 @@
         functools.partial(number_kernel, logits.shape[1]), 1, S((2, rows), jnp.int32), 1 * MIB, cost=hint
     )(routes.T)
     routed = []
-    for offsets in plan:
+    for offsets in plan[:whole]:
         routed.append(exchange(numbers, devices, offsets))
     weights, coefs = call(
         functools.partial(route_kernel, [(0, 0), (last, last)], plan, segments), 2,
         [S((rows, 128), f32), S((2 * rows, count * rows), bf16)], 1 * MIB,
     )(routes, logits)
-    picks = call(functools.partial(select_kernel, segments), count, S((count * rows, rows), bf16), 1 * MIB)(*routed)
+    picks = call(functools.partial(select_kernel, segments), whole, S((whole * rows, rows), bf16), 1 * MIB)(*routed)
     theirs = []
     for m in mine:
         theirs.append(swap_cores(m))
     total, cut = (2 * count + 2) * rows, (count + 2) * rows
     keep, give = call(
         functools.partial(hidden_kernel, count), 2 * count + 4,
-        [S((cut, hidden), bf16)] * 2, 14 * MIB, [pltpu.VMEM((total, width), bf16)],
+        [S((cut, hidden), bf16)] * 2, 12 * MIB + 8 * total * width,
+        [pltpu.VMEM((total, width), bf16)] + [spread] * (2 * (count - whole)),
     )(tokens, *mine, near, *theirs, gate, up)
     got = swap_cores(give)
-    slots = S((BASE, width * CAP // BASE), bf16)
-    spare, spread = pltpu.VMEM((BASE, width // BASE), f32), pltpu.VMEM((rows, width), f32)
     begun = call(
-        functools.partial(first_kernel, count), 3, S((cut, width), f32), 8 * MIB,
+        first_kernel, 3, S((cut, width), f32), 8 * MIB,
         [pltpu.VMEM((cut, hidden), bf16)],
     )(keep, picks, down)
     *outs, out_half, own = call(
@@ -264,7 +309,7 @@
 
 
 def solution(mesh):
-    return jax.shard_map(
+    step = jax.shard_map(
         layer,
         mesh=mesh,
         in_specs=(
@@ -278,3 +323,5 @@
         out_specs=P(("groups", "expert"), "tensor"),
         check_vma=False,
     )
+    _, _, _ = partner_plan(mesh.shape["expert"])
+    return step

time: 46.2 us -> 36.6 us (0.79)
  local copies, waits for them, and re-layouts: 4.85 us -> 0.19 us
  starting transfers between devices: 20.9 us -> 17.7 us
  waiting for transfers between devices: 16 us -> 14 us
    unnamed x14, local copies, waits for them, and re-layouts: 4.85 us -> 0.19 us
    ppermute x11 -> x9, starting transfers between devices: 17.7 us -> 15.8 us  [exchange(): return lax.ppermute(x, AXES, pairs)]
    ppermute x11 -> x9, waiting for transfers between devices: 15.2 us -> 13.8 us  [exchange(): return lax.ppermute(x, AXES, pairs)]
    ppermute x6, starting transfers between devices: 3.25 us -> 1.92 us  [swap_cores(): return lax.ppermute(x, 'tensor', [(0, 1), (1, 0)])]
    ppermute x6, waiting for transfers between devices: 0.75 us -> 0.16 us  [swap_cores(): return lax.ppermute(x, 'tensor', [(0, 1), (1, 0)])]
    pallas_call x2 -> x4, Pallas kernels: 0.75 us -> 1.09 us  [the longest x1 0.74 us: layer(): call(first_kernel, 3, S((cut, width), f32), 8 * MIB, [pltpu.VMEM((cut, hi...]
  transfers between devices with their start and end apart: 17 -> 15, of which waited for: 8 -> 8; matrix products, arithmetic and copies ran while one was open for 0% -> 0% of each run, Pallas kernels for 5% -> 8%
where the time goes in v3:
time: 36.6 us; the launch traced here: 36.4 us
  starting transfers between devices  17.7 us (48%)
  waiting for transfers between devices  14 us (38%)
  Pallas kernels  4.52 us (12%)
    ppermute x9, starting transfers between devices, exchange(): return lax.ppermute(x, AXES, pairs)  15.8 us
    ppermute x9, waiting for transfers between devices, exchange(): return lax.ppermute(x, AXES, pairs)  13.8 us
    ppermute x6, starting transfers between devices, swap_cores(): return lax.ppermute(x, 'tensor', [(0, 1), (1, 0)])  1.92 us
    pallas_call x1, Pallas kernels, layer(): call(functools.partial(hidden_kernel, count), 2 * count + 4, [S((cut, hid...  1.24 us
    pallas_call x1, Pallas kernels, layer(): call(functools.partial(down_kernel, count), 4, [slots] * count + [S((rows...  0.77 us
    pallas_call x1, Pallas kernels, layer(): call(first_kernel, 3, S((cut, width), f32), 8 * MIB, [pltpu.VMEM((cut, hi...  0.74 us
  transfers between devices with their start and end apart: 15, of which 8 were waited for; matrix products, arithmetic and copies ran while one was open for 0% of the time, Pallas kernels for 8%

profile of v3, /device:TPU:0, one launch (start us, length us, event | category | flops | bytes accessed | tf_op | source)
XLA Modules:
  0.0 36.4 jit_solution(3261308728060556029)
XLA Ops:
  0.0 0.6 %collective-permute-start.9 = (bf16[1,256,6144]{2,1,0:T(8,128)(2,1)}, bf16[1,256,6144]{2,1,0:T(8,128)(2,1)S(1)}, u32[]{:S(2)}, u32[]{:S(2)}) collective-permute-start(bf16[1,256,6144]{2,1,0:T(8,128)(2,1)} %down.1), channel_id=1, source_target_pairs={{0,1},{1,0},{2,3},{3,2},{4,5},{5,4},{6,7},{7,6},{8,9},{9,8},{10,11... | collective-permute-start | bytes 9437192 | tf_op jit(solution)/shard_map/ppermute | solution.py:35
  0.6 2.6 %collective-permute-start = (bf16[8,6144]{1,0:T(8,128)(2,1)}, bf16[8,6144]{1,0:T(8,128)(2,1)S(1)}, u32[]{:S(2)}, u32[]{:S(2)}) collective-permute-start(bf16[8,6144]{1,0:T(8,128)(2,1)} %refs_0_.1), channel_id=1, source_target_pairs={{0,4},{1,13},{2,6},{3,15},{4,0},{5,9},{6,2},{7,11},{8,12},{9,5},{1... | collective-permute-start | bytes 294920 | tf_op jit(solution)/shard_map/ppermute | solution.py:31
  3.2 0.3 shard_map.66
  3.6 3.6 %collective-permute-start.1 = (bf16[4,7680]{1,0:T(4,128)(2,1)S(1)}, bf16[4,7680]{1,0:T(4,128)(2,1)S(1)}, u32[]{:S(2)}, u32[]{:S(2)}) collective-permute-start(bf16[4,7680]{1,0:T(4,128)(2,1)S(1)} %get-tuple-element.20), channel_id=1, source_target_pairs={{0,10},{1,9},{2,8},{3,11},{4,14},{5,13},{6,12},{7,15},{8,2},{9,1},... | collective-permute-start | bytes 184328 | tf_op jit(solution)/shard_map/ppermute | solution.py:31
  7.2 0.7 %collective-permute-start.2 = (bf16[4,7680]{1,0:T(4,128)(2,1)S(1)}, bf16[4,7680]{1,0:T(4,128)(2,1)S(1)}, u32[]{:S(2)}, u32[]{:S(2)}) collective-permute-start(bf16[4,7680]{1,0:T(4,128)(2,1)S(1)} %get-tuple-element.21), channel_id=1, source_target_pairs={{0,6},{1,15},{2,4},{3,13},{4,2},{5,11},{6,0},{7,9},{8,14},{9,7},{1... | collective-permute-start | bytes 184328 | tf_op jit(solution)/shard_map/ppermute | solution.py:31
  7.8 1.5 %collective-permute-start.3 = (bf16[8,6144]{1,0:T(8,128)(2,1)S(1)}, bf16[8,6144]{1,0:T(8,128)(2,1)S(1)}, u32[]{:S(2)}, u32[]{:S(2)}) collective-permute-start(bf16[8,6144]{1,0:T(8,128)(2,1)S(1)} %copy-done.3), channel_id=1, source_target_pairs={{0,2},{1,3},{2,0},{3,1},{4,6},{5,7},{6,4},{7,5},{8,10},{9,11},{10,... | collective-permute-start | bytes 294920 | tf_op jit(solution)/shard_map/ppermute | solution.py:31
  9.4 0.8 %collective-permute-done.1.refs_2_ = bf16[4,7680]{1,0:T(4,128)(2,1)S(1)} collective-permute-done((bf16[4,7680]{1,0:T(4,128)(2,1)S(1)}, bf16[4,7680]{1,0:T(4,128)(2,1)S(1)}, u32[]{:S(2)}, u32[]{:S(2)}) %collective-permute-start.1) | collective-permute-done | bytes 61472 | tf_op jit(solution)/shard_map/ppermute | solution.py:31
  10.2 1.1 %collective-permute-start.5 = (bf16[4,7680]{1,0:T(4,128)(2,1)S(1)}, bf16[4,7680]{1,0:T(4,128)(2,1)S(1)}, u32[]{:S(2)}, u32[]{:S(2)}) collective-permute-start(bf16[4,7680]{1,0:T(4,128)(2,1)S(1)} %collective-permute-done.1.refs_2_), channel_id=1, source_target_pairs={{0,1},{1,0},{2,3},{3,2},{4,5},{5,4},{6,7},{7,6},{8,9},{9,8},{10,11... | collective-permute-start | bytes 184328 | tf_op jit(solution)/shard_map/ppermute | solution.py:35
  11.2 1.8 %collective-permute-done.2.refs_3_ = bf16[4,7680]{1,0:T(4,128)(2,1)S(1)} collective-permute-done((bf16[4,7680]{1,0:T(4,128)(2,1)S(1)}, bf16[4,7680]{1,0:T(4,128)(2,1)S(1)}, u32[]{:S(2)}, u32[]{:S(2)}) %collective-permute-start.2) | collective-permute-done | bytes 61472 | tf_op jit(solution)/shard_map/ppermute | solution.py:31
  13.0 1.1 %collective-permute-done.3.refs_4_ = bf16[8,6144]{1,0:T(8,128)(2,1)S(1)} collective-permute-done((bf16[8,6144]{1,0:T(8,128)(2,1)S(1)}, bf16[8,6144]{1,0:T(8,128)(2,1)S(1)}, u32[]{:S(2)}, u32[]{:S(2)}) %collective-permute-start.3) | collective-permute-done | bytes 98336 | tf_op jit(solution)/shard_map/ppermute | solution.py:31
  14.3 1.2 %shard_map.67 = (bf16[40,256]{1,0:T(8,128)(2,1)S(1)}, bf16[40,256]{1,0:T(8,128)(2,1)S(1)}) custom-call(bf16[8,6144]{1,0:T(8,128)(2,1)S(1)} %copy-done.3, bf16[8,6144]{1,0:T(8,128)(2,1)S(1)} %collective-permute-done.refs_1_, bf16[4,7680]{1,0:T(4,128)(2,1)S(1)} %collective-permute-done.1.refs_2_, bf16[4,7680]{1,0:T(4,128)(2,1)S(1)} %collective-permute-done.2.refs_3_, ...), custom_call_target="tpu_custom_call" | custom-call | tf_op jit(solution)/shard_map/pallas_call | solution.py:283
  15.9 1.3 %collective-permute-start.8 = (s32[2,8]{1,0:T(2,128)S(1)}, s32[2,8]{1,0:T(2,128)S(1)}, u32[]{:S(2)}, u32[]{:S(2)}) collective-permute-start(s32[2,8]{1,0:T(2,128)S(1)} %shard_map.68), channel_id=1, source_target_pairs={{0,4},{1,13},{2,6},{3,15},{4,0},{5,9},{6,2},{7,11},{8,12},{9,5},{1... | collective-permute-start | bytes 200 | tf_op jit(solution)/shard_map/ppermute | solution.py:31
  17.2 2.3 %collective-permute-done.8.refs_0_ = s32[2,8]{1,0:T(2,128)S(1)} collective-permute-done((s32[2,8]{1,0:T(2,128)S(1)}, s32[2,8]{1,0:T(2,128)S(1)}, u32[]{:S(2)}, u32[]{:S(2)}) %collective-permute-start.8) | collective-permute-done | bytes 96 | tf_op jit(solution)/shard_map/ppermute | solution.py:31
  19.5 0.7 %shard_map.70.begun = f32[40,6144]{1,0:T(8,128)S(1)} custom-call(bf16[40,256]{1,0:T(8,128)(2,1)S(1)} %get-tuple-element.23.mine, bf16[8,8]{1,0:T(8,128)(2,1)S(1)} %shard_map.69.picks, bf16[1,256,6144]{2,1,0:T(8,128)(2,1)S(1)} %copy-done.2), custom_call_target="tpu_custom_call" | custom-call | tf_op jit(solution)/shard_map/pallas_call | solution.py:289
  20.3 0.8 %shard_map.71 = (bf16[4,7680]{1,0:T(4,128)(2,1)S(1)}, bf16[4,7680]{1,0:T(4,128)(2,1)S(1)}, bf16[4,7680]{1,0:T(4,128)(2,1)S(1)}, bf16[8,3072]{1,0:T(8,128)(2,1)S(1)}, f32[8,3072]{1,0:T(8,128)S(1)}) custom-call(bf16[40,256]{1,0:T(8,128)(2,1)S(1)} %collective-permute-done.7.theirs, bf16[8,8]{1,0:T(8,128)(2,1)S(1)} %shard_map.69.picks, ...), custom_call_target="tpu_custom_call" | custom-call | tf_op jit(solution)/shard_map/pallas_call | solution.py:293
  21.1 1.4 %collective-permute-start.10 = (bf16[4,7680]{1,0:T(4,128)(2,1)S(1)}, bf16[4,7680]{1,0:T(4,128)(2,1)S(1)}, u32[]{:S(2)}, u32[]{:S(2)}) collective-permute-start(bf16[4,7680]{1,0:T(4,128)(2,1)S(1)} %get-tuple-element.25), channel_id=1, source_target_pairs={{0,4},{1,13},{2,6},{3,15},{4,0},{5,9},{6,2},{7,11},{8,12},{9,5},{1... | collective-permute-start | bytes 184328 | tf_op jit(solution)/shard_map/ppermute | solution.py:31
  22.4 1.8 %collective-permute-start.11 = (bf16[4,7680]{1,0:T(4,128)(2,1)S(1)}, bf16[4,7680]{1,0:T(4,128)(2,1)S(1)}, u32[]{:S(2)}, u32[]{:S(2)}) collective-permute-start(bf16[4,7680]{1,0:T(4,128)(2,1)S(1)} %get-tuple-element.26), channel_id=1, source_target_pairs={{0,10},{1,9},{2,8},{3,11},{4,14},{5,13},{6,12},{7,15},{8,2},{9,1},... | collective-permute-start | bytes 184328 | tf_op jit(solution)/shard_map/ppermute | solution.py:31
  24.2 1.4 %collective-permute-start.12 = (bf16[4,7680]{1,0:T(4,128)(2,1)S(1)}, bf16[4,7680]{1,0:T(4,128)(2,1)S(1)}, u32[]{:S(2)}, u32[]{:S(2)}) collective-permute-start(bf16[4,7680]{1,0:T(4,128)(2,1)S(1)} %get-tuple-element.27), channel_id=1, source_target_pairs={{0,6},{1,15},{2,4},{3,13},{4,2},{5,11},{6,0},{7,9},{8,14},{9,7},{1... | collective-permute-start | bytes 184328 | tf_op jit(solution)/shard_map/ppermute | solution.py:31
  25.8 0.3 shard_map.64
  26.2 4.9 %collective-permute-done.11.refs_1_ = bf16[4,7680]{1,0:T(4,128)(2,1)S(1)} collective-permute-done((bf16[4,7680]{1,0:T(4,128)(2,1)S(1)}, bf16[4,7680]{1,0:T(4,128)(2,1)S(1)}, u32[]{:S(2)}, u32[]{:S(2)}) %collective-permute-start.11) | collective-permute-done | bytes 61472 | tf_op jit(solution)/shard_map/ppermute | solution.py:31
  31.2 0.3 shard_map.72
  31.6 1.4 %collective-permute-start.14 = (bf16[8,3072]{1,0:T(8,128)(2,1)S(1)}, bf16[8,3072]{1,0:T(8,128)(2,1)S(1)}, u32[]{:S(2)}, u32[]{:S(2)}) collective-permute-start(bf16[8,3072]{1,0:T(8,128)(2,1)S(1)} %get-tuple-element.30), channel_id=1, source_target_pairs={{0,2},{1,3},{2,0},{3,1},{4,6},{5,7},{6,4},{7,5},{8,10},{9,11},{10,... | collective-permute-start | bytes 147464 | tf_op jit(solution)/shard_map/ppermute | solution.py:31
  33.0 2.7 %collective-permute-done.14.back_half = bf16[8,3072]{1,0:T(8,128)(2,1)S(1)} collective-permute-done((bf16[8,3072]{1,0:T(8,128)(2,1)S(1)}, bf16[8,3072]{1,0:T(8,128)(2,1)S(1)}, u32[]{:S(2)}, u32[]{:S(2)}) %collective-permute-start.14) | collective-permute-done | bytes 49184 | tf_op jit(solution)/shard_map/ppermute | solution.py:31
  35.7 0.7 %shard_map.73 = bf16[8,3072]{1,0:T(8,128)(2,1)} custom-call(f32[8,128]{1,0:T(8,128)S(1)} %get-tuple-element.18.weights, f32[8,3072]{1,0:T(8,128)S(1)} %get-tuple-element.28.keep, f32[8,3072]{1,0:T(8,128)S(1)} %collective-permute-done.13.got, bf16[8,3072]{1,0:T(8,128)(2,1)S(1)} %collective-permute-done.14.back_half), custom_call_target="tpu_custom_call" | custom-call | tf_op jit(solution)/shard_map/pallas_call | solution.py:308
  (30 shorter events, 1.0 us)
Async XLA Ops:
  0.0 3.2 %copy-start.3 = (bf16[8,6144]{1,0:T(8,128)(2,1)S(1)}, bf16[8,6144]{1,0:T(8,128)(2,1)}, u32[]{:S(2)}) copy-start(bf16[8,6144]{1,0:T(8,128)(2,1)} %refs_0_.1) | copy-start | bytes 294916
  0.0 3.2 %copy-start.4 = (s32[8,2]{0,1:T(2,128)S(1)}, s32[8,2]{0,1:T(2,128)}, u32[]{:S(2)}) copy-start(s32[8,2]{0,1:T(2,128)} %param.7) | copy-start | bytes 196
  0.0 14.3 %copy-start.1 = (bf16[1,6144,256]{2,1,0:T(8,128)(2,1)S(1)}, bf16[1,6144,256]{2,1,0:T(8,128)(2,1)}, u32[]{:S(2)}) copy-start(bf16[1,6144,256]{2,1,0:T(8,128)(2,1)} %refs_9_.1) | copy-start | bytes 9437188
  0.0 14.3 %copy-start = (bf16[1,6144,256]{2,1,0:T(8,128)(2,1)S(1)}, bf16[1,6144,256]{2,1,0:T(8,128)(2,1)}, u32[]{:S(2)}) copy-start(bf16[1,6144,256]{2,1,0:T(8,128)(2,1)} %refs_8_.1) | copy-start | bytes 9437188
  0.0 20.3 %collective-permute-start.9 = (bf16[1,256,6144]{2,1,0:T(8,128)(2,1)}, bf16[1,256,6144]{2,1,0:T(8,128)(2,1)S(1)}, u32[]{:S(2)}, u32[]{:S(2)}) collective-permute-start(bf16[1,256,6144]{2,1,0:T(8,128)(2,1)} %down.1), channel_id=1, source_target_pairs={{0,1},{1,0},{2,3},{3,2},{4,5},{5,4},{6,7},{7,6},{8,9},{9,8},{10,11... | collective-permute-start | bytes 9437192 | tf_op jit(solution)/shard_map/ppermute | solution.py:35
  0.6 8.8 %collective-permute-start = (bf16[8,6144]{1,0:T(8,128)(2,1)}, bf16[8,6144]{1,0:T(8,128)(2,1)S(1)}, u32[]{:S(2)}, u32[]{:S(2)}) collective-permute-start(bf16[8,6144]{1,0:T(8,128)(2,1)} %refs_0_.1), channel_id=1, source_target_pairs={{0,4},{1,13},{2,6},{3,15},{4,0},{5,9},{6,2},{7,11},{8,12},{9,5},{1... | collective-permute-start | bytes 294920 | tf_op jit(solution)/shard_map/ppermute | solution.py:31
  3.6 6.6 %collective-permute-start.1 = (bf16[4,7680]{1,0:T(4,128)(2,1)S(1)}, bf16[4,7680]{1,0:T(4,128)(2,1)S(1)}, u32[]{:S(2)}, u32[]{:S(2)}) collective-permute-start(bf16[4,7680]{1,0:T(4,128)(2,1)S(1)} %get-tuple-element.20), channel_id=1, source_target_pairs={{0,10},{1,9},{2,8},{3,11},{4,14},{5,13},{6,12},{7,15},{8,2},{9,1},... | collective-permute-start | bytes 184328 | tf_op jit(solution)/shard_map/ppermute | solution.py:31
  7.2 5.9 %collective-permute-start.2 = (bf16[4,7680]{1,0:T(4,128)(2,1)S(1)}, bf16[4,7680]{1,0:T(4,128)(2,1)S(1)}, u32[]{:S(2)}, u32[]{:S(2)}) collective-permute-start(bf16[4,7680]{1,0:T(4,128)(2,1)S(1)} %get-tuple-element.21), channel_id=1, source_target_pairs={{0,6},{1,15},{2,4},{3,13},{4,2},{5,11},{6,0},{7,9},{8,14},{9,7},{1... | collective-permute-start | bytes 184328 | tf_op jit(solution)/shard_map/ppermute | solution.py:31
  7.8 6.3 %collective-permute-start.3 = (bf16[8,6144]{1,0:T(8,128)(2,1)S(1)}, bf16[8,6144]{1,0:T(8,128)(2,1)S(1)}, u32[]{:S(2)}, u32[]{:S(2)}) collective-permute-start(bf16[8,6144]{1,0:T(8,128)(2,1)S(1)} %copy-done.3), channel_id=1, source_target_pairs={{0,2},{1,3},{2,0},{3,1},{4,6},{5,7},{6,4},{7,5},{8,10},{9,11},{10,... | collective-permute-start | bytes 294920 | tf_op jit(solution)/shard_map/ppermute | solution.py:31
  9.4 4.9 %collective-permute-start.4 = (bf16[8,6144]{1,0:T(8,128)(2,1)S(1)}, bf16[8,6144]{1,0:T(8,128)(2,1)S(1)}, u32[]{:S(2)}, u32[]{:S(2)}) collective-permute-start(bf16[8,6144]{1,0:T(8,128)(2,1)S(1)} %collective-permute-done.refs_1_), channel_id=1, source_target_pairs={{0,1},{1,0},{2,3},{3,2},{4,5},{5,4},{6,7},{7,6},{8,9},{9,8},{10,11... | collective-permute-start | bytes 294920 | tf_op jit(solution)/shard_map/ppermute | solution.py:35
  10.2 4.0 %collective-permute-start.5 = (bf16[4,7680]{1,0:T(4,128)(2,1)S(1)}, bf16[4,7680]{1,0:T(4,128)(2,1)S(1)}, u32[]{:S(2)}, u32[]{:S(2)}) collective-permute-start(bf16[4,7680]{1,0:T(4,128)(2,1)S(1)} %collective-permute-done.1.refs_2_), channel_id=1, source_target_pairs={{0,1},{1,0},{2,3},{3,2},{4,5},{5,4},{6,7},{7,6},{8,9},{9,8},{10,11... | collective-permute-start | bytes 184328 | tf_op jit(solution)/shard_map/ppermute | solution.py:35
  13.0 1.2 %collective-permute-start.6 = (bf16[4,7680]{1,0:T(4,128)(2,1)S(1)}, bf16[4,7680]{1,0:T(4,128)(2,1)S(1)}, u32[]{:S(2)}, u32[]{:S(2)}) collective-permute-start(bf16[4,7680]{1,0:T(4,128)(2,1)S(1)} %collective-permute-done.2.refs_3_), channel_id=1, source_target_pairs={{0,1},{1,0},{2,3},{3,2},{4,5},{5,4},{6,7},{7,6},{8,9},{9,8},{10,11... | collective-permute-start | bytes 184328 | tf_op jit(solution)/shard_map/ppermute | solution.py:35
  15.5 4.0 %copy-start.2 = (bf16[1,256,6144]{2,1,0:T(8,128)(2,1)S(1)}, bf16[1,256,6144]{2,1,0:T(8,128)(2,1)}, u32[]{:S(2)}) copy-start(bf16[1,256,6144]{2,1,0:T(8,128)(2,1)} %down.1) | copy-start | bytes 9437188
  15.6 4.7 %collective-permute-start.7 = (bf16[40,256]{1,0:T(8,128)(2,1)S(1)}, bf16[40,256]{1,0:T(8,128)(2,1)S(1)}, u32[]{:S(2)}, u32[]{:S(2)}) collective-permute-start(bf16[40,256]{1,0:T(8,128)(2,1)S(1)} %get-tuple-element.22), channel_id=1, source_target_pairs={{0,1},{1,0},{2,3},{3,2},{4,5},{5,4},{6,7},{7,6},{8,9},{9,8},{10,11... | collective-permute-start | bytes 61448 | tf_op jit(solution)/shard_map/ppermute | solution.py:35
  15.9 3.6 %collective-permute-start.8 = (s32[2,8]{1,0:T(2,128)S(1)}, s32[2,8]{1,0:T(2,128)S(1)}, u32[]{:S(2)}, u32[]{:S(2)}) collective-permute-start(s32[2,8]{1,0:T(2,128)S(1)} %shard_map.68), channel_id=1, source_target_pairs={{0,4},{1,13},{2,6},{3,15},{4,0},{5,9},{6,2},{7,11},{8,12},{9,5},{1... | collective-permute-start | bytes 200 | tf_op jit(solution)/shard_map/ppermute | solution.py:31
  19.5 6.2 %copy-start.5 = (f32[8,4]{0,1:T(4,128)S(1)}, f32[8,4]{0,1:T(4,128)}, u32[]{:S(2)}) copy-start(f32[8,4]{0,1:T(4,128)} %param.8) | copy-start | bytes 388
  21.1 5.1 %collective-permute-start.10 = (bf16[4,7680]{1,0:T(4,128)(2,1)S(1)}, bf16[4,7680]{1,0:T(4,128)(2,1)S(1)}, u32[]{:S(2)}, u32[]{:S(2)}) collective-permute-start(bf16[4,7680]{1,0:T(4,128)(2,1)S(1)} %get-tuple-element.25), channel_id=1, source_target_pairs={{0,4},{1,13},{2,6},{3,15},{4,0},{5,9},{6,2},{7,11},{8,12},{9,5},{1... | collective-permute-start | bytes 184328 | tf_op jit(solution)/shard_map/ppermute | solution.py:31
  22.4 8.6 %collective-permute-start.11 = (bf16[4,7680]{1,0:T(4,128)(2,1)S(1)}, bf16[4,7680]{1,0:T(4,128)(2,1)S(1)}, u32[]{:S(2)}, u32[]{:S(2)}) collective-permute-start(bf16[4,7680]{1,0:T(4,128)(2,1)S(1)} %get-tuple-element.26), channel_id=1, source_target_pairs={{0,10},{1,9},{2,8},{3,11},{4,14},{5,13},{6,12},{7,15},{8,2},{9,1},... | collective-permute-start | bytes 184328 | tf_op jit(solution)/shard_map/ppermute | solution.py:31
  24.2 7.0 %collective-permute-start.12 = (bf16[4,7680]{1,0:T(4,128)(2,1)S(1)}, bf16[4,7680]{1,0:T(4,128)(2,1)S(1)}, u32[]{:S(2)}, u32[]{:S(2)}) collective-permute-start(bf16[4,7680]{1,0:T(4,128)(2,1)S(1)} %get-tuple-element.27), channel_id=1, source_target_pairs={{0,6},{1,15},{2,4},{3,13},{4,2},{5,11},{6,0},{7,9},{8,14},{9,7},{1... | collective-permute-start | bytes 184328 | tf_op jit(solution)/shard_map/ppermute | solution.py:31
  31.5 4.2 %collective-permute-start.13 = (f32[8,3072]{1,0:T(8,128)S(1)}, f32[8,3072]{1,0:T(8,128)S(1)}, u32[]{:S(2)}, u32[]{:S(2)}) collective-permute-start(f32[8,3072]{1,0:T(8,128)S(1)} %get-tuple-element.29), channel_id=1, source_target_pairs={{0,1},{1,0},{2,3},{3,2},{4,5},{5,4},{6,7},{7,6},{8,9},{9,8},{10,11... | collective-permute-start | bytes 294920 | tf_op jit(solution)/shard_map/ppermute | solution.py:35
  31.6 4.2 %collective-permute-start.14 = (bf16[8,3072]{1,0:T(8,128)(2,1)S(1)}, bf16[8,3072]{1,0:T(8,128)(2,1)S(1)}, u32[]{:S(2)}, u32[]{:S(2)}) collective-permute-start(bf16[8,3072]{1,0:T(8,128)(2,1)S(1)} %get-tuple-element.30), channel_id=1, source_target_pairs={{0,2},{1,3},{2,0},{3,1},{4,6},{5,7},{6,4},{7,5},{8,10},{9,11},{10,... | collective-permute-start | bytes 147464 | tf_op jit(solution)/shard_map/ppermute | solution.py:31

commit v4 on v3

--- a/solution.py
+++ b/solution.py
@@ -233,11 +233,11 @@
     mixed = jnp.dot(coefs[...], stack[...], preferred_element_type=F32)
     total[...] = mixed[:rows] + mixed[rows:]
     keep[...] = total[:, pl.ds(here, half)] + weights[:, 0:1] * own[...]
-    give[...] = total[:, pl.ds(there, half)]
+    give[...] = total[:, pl.ds(there, half)].astype(BF16)
 
 
 def last_kernel(weights, keep, got, back_half, out):
-    total = keep[...] + got[...] + weights[:, 1:2] * back_half[...].astype(F32)
+    total = keep[...] + got[...].astype(F32) + weights[:, 1:2] * back_half[...].astype(F32)
     out[...] = total.astype(BF16)
 
 
@@ -300,7 +300,7 @@
         back.append(exchange(o, devices, offsets))
     back, back_half = back[:-1], back[-1]
     keep, give = call(
-        functools.partial(mix_kernel, count), count + 3, [S((rows, half), f32)] * 2,
+        functools.partial(mix_kernel, count), count + 3, [S((rows, half), f32), S((rows, half), bf16)],
         4 * MIB + count * MIB,
         [pltpu.VMEM((count * rows, width), bf16), spread] + [spread] * count,
     )(weights, coefs, own, *back)

time: 36.6 us -> 33.6 us (0.918)
  waiting for transfers between devices: 14 us -> 11.8 us
  starting transfers between devices: 17.7 us -> 16.9 us
    ppermute x9, waiting for transfers between devices: 13.8 us -> 10.6 us  [exchange(): return lax.ppermute(x, AXES, pairs)]
    ppermute x6, waiting for transfers between devices: 0.16 us -> 1.29 us  [swap_cores(): return lax.ppermute(x, 'tensor', [(0, 1), (1, 0)])]
    ppermute x9, starting transfers between devices: 15.8 us -> 14.9 us  [exchange(): return lax.ppermute(x, AXES, pairs)]
  transfers between devices with their start and end apart: 15 -> 15, of which waited for: 8 -> 9; matrix products, arithmetic and copies ran while one was open for 0% -> 0% of each run, Pallas kernels for 8% -> 9%
where the time goes in v4:
time: 33.6 us; the launch traced here: 33.5 us
  starting transfers between devices  16.9 us (50%)
  waiting for transfers between devices  11.8 us (35%)
  Pallas kernels  4.51 us (13%)
    ppermute x9, starting transfers between devices, exchange(): return lax.ppermute(x, AXES, pairs)  14.9 us
    ppermute x9, waiting for transfers between devices, exchange(): return lax.ppermute(x, AXES, pairs)  10.6 us
    ppermute x6, starting transfers between devices, swap_cores(): return lax.ppermute(x, 'tensor', [(0, 1), (1, 0)])  1.92 us
    ppermute x6, waiting for transfers between devices, swap_cores(): return lax.ppermute(x, 'tensor', [(0, 1), (1, 0)])  1.29 us
    pallas_call x1, Pallas kernels, layer(): call(functools.partial(hidden_kernel, count), 2 * count + 4, [S((cut, hid...  1.24 us
    pallas_call x1, Pallas kernels, layer(): call(functools.partial(down_kernel, count), 4, [slots] * count + [S((rows...  0.77 us
    pallas_call x1, Pallas kernels, layer(): call(first_kernel, 3, S((cut, width), f32), 8 * MIB, [pltpu.VMEM((cut, hi...  0.74 us
    pallas_call x1, Pallas kernels, layer(): call(last_kernel, 4, S((rows, half), bf16), 4 * MIB)  0.7 us
  transfers between devices with their start and end apart: 15, of which 9 were waited for; matrix products, arithmetic and copies ran while one was open for 0% of the time, Pallas kernels for 9%

profile of v4, /device:TPU:0, one launch (start us, length us, event | category | flops | bytes accessed | tf_op | source)
XLA Modules:
  0.0 33.5 jit_solution(14197632064953782860)
XLA Ops:
  0.0 0.6 %collective-permute-start.9 = (bf16[1,256,6144]{2,1,0:T(8,128)(2,1)}, bf16[1,256,6144]{2,1,0:T(8,128)(2,1)S(1)}, u32[]{:S(2)}, u32[]{:S(2)}) collective-permute-start(bf16[1,256,6144]{2,1,0:T(8,128)(2,1)} %down.1), channel_id=1, source_target_pairs={{0,1},{1,0},{2,3},{3,2},{4,5},{5,4},{6,7},{7,6},{8,9},{9,8},{10,11... | collective-permute-start | bytes 9437192 | tf_op jit(solution)/shard_map/ppermute | solution.py:35
  0.6 2.6 %collective-permute-start = (bf16[8,6144]{1,0:T(8,128)(2,1)}, bf16[8,6144]{1,0:T(8,128)(2,1)S(1)}, u32[]{:S(2)}, u32[]{:S(2)}) collective-permute-start(bf16[8,6144]{1,0:T(8,128)(2,1)} %refs_0_.1), channel_id=1, source_target_pairs={{0,4},{1,13},{2,6},{3,15},{4,0},{5,9},{6,2},{7,11},{8,12},{9,5},{1... | collective-permute-start | bytes 294920 | tf_op jit(solution)/shard_map/ppermute | solution.py:31
  3.2 0.3 %shard_map.66 = (bf16[4,7680]{1,0:T(4,128)(2,1)S(1)}, bf16[4,7680]{1,0:T(4,128)(2,1)S(1)}) custom-call(bf16[8,6144]{1,0:T(8,128)(2,1)S(1)} %copy-done.3, s32[2,8]{1,0:T(2,128)S(1)} %bitcast.1, bf16[8,8]{1,0:T(8,128)(2,1)S(1)} %shard_map.65.before), custom_call_target="tpu_custom_call" | custom-call | tf_op jit(solution)/shard_map/pallas_call | solution.py:257
  3.6 3.6 %collective-permute-start.1 = (bf16[4,7680]{1,0:T(4,128)(2,1)S(1)}, bf16[4,7680]{1,0:T(4,128)(2,1)S(1)}, u32[]{:S(2)}, u32[]{:S(2)}) collective-permute-start(bf16[4,7680]{1,0:T(4,128)(2,1)S(1)} %get-tuple-element.20), channel_id=1, source_target_pairs={{0,10},{1,9},{2,8},{3,11},{4,14},{5,13},{6,12},{7,15},{8,2},{9,1},... | collective-permute-start | bytes 184328 | tf_op jit(solution)/shard_map/ppermute | solution.py:31
  7.2 0.7 %collective-permute-start.2 = (bf16[4,7680]{1,0:T(4,128)(2,1)S(1)}, bf16[4,7680]{1,0:T(4,128)(2,1)S(1)}, u32[]{:S(2)}, u32[]{:S(2)}) collective-permute-start(bf16[4,7680]{1,0:T(4,128)(2,1)S(1)} %get-tuple-element.21), channel_id=1, source_target_pairs={{0,6},{1,15},{2,4},{3,13},{4,2},{5,11},{6,0},{7,9},{8,14},{9,7},{1... | collective-permute-start | bytes 184328 | tf_op jit(solution)/shard_map/ppermute | solution.py:31
  7.8 1.5 %collective-permute-start.3 = (bf16[8,6144]{1,0:T(8,128)(2,1)S(1)}, bf16[8,6144]{1,0:T(8,128)(2,1)S(1)}, u32[]{:S(2)}, u32[]{:S(2)}) collective-permute-start(bf16[8,6144]{1,0:T(8,128)(2,1)S(1)} %copy-done.3), channel_id=1, source_target_pairs={{0,2},{1,3},{2,0},{3,1},{4,6},{5,7},{6,4},{7,5},{8,10},{9,11},{10,... | collective-permute-start | bytes 294920 | tf_op jit(solution)/shard_map/ppermute | solution.py:31
  9.4 0.8 %collective-permute-done.1.refs_2_ = bf16[4,7680]{1,0:T(4,128)(2,1)S(1)} collective-permute-done((bf16[4,7680]{1,0:T(4,128)(2,1)S(1)}, bf16[4,7680]{1,0:T(4,128)(2,1)S(1)}, u32[]{:S(2)}, u32[]{:S(2)}) %collective-permute-start.1) | collective-permute-done | bytes 61472 | tf_op jit(solution)/shard_map/ppermute | solution.py:31
  10.2 1.1 %collective-permute-start.5 = (bf16[4,7680]{1,0:T(4,128)(2,1)S(1)}, bf16[4,7680]{1,0:T(4,128)(2,1)S(1)}, u32[]{:S(2)}, u32[]{:S(2)}) collective-permute-start(bf16[4,7680]{1,0:T(4,128)(2,1)S(1)} %collective-permute-done.1.refs_2_), channel_id=1, source_target_pairs={{0,1},{1,0},{2,3},{3,2},{4,5},{5,4},{6,7},{7,6},{8,9},{9,8},{10,11... | collective-permute-start | bytes 184328 | tf_op jit(solution)/shard_map/ppermute | solution.py:35
  11.2 1.8 %collective-permute-done.2.refs_3_ = bf16[4,7680]{1,0:T(4,128)(2,1)S(1)} collective-permute-done((bf16[4,7680]{1,0:T(4,128)(2,1)S(1)}, bf16[4,7680]{1,0:T(4,128)(2,1)S(1)}, u32[]{:S(2)}, u32[]{:S(2)}) %collective-permute-start.2) | collective-permute-done | bytes 61472 | tf_op jit(solution)/shard_map/ppermute | solution.py:31
  13.0 1.1 %collective-permute-done.3.refs_4_ = bf16[8,6144]{1,0:T(8,128)(2,1)S(1)} collective-permute-done((bf16[8,6144]{1,0:T(8,128)(2,1)S(1)}, bf16[8,6144]{1,0:T(8,128)(2,1)S(1)}, u32[]{:S(2)}, u32[]{:S(2)}) %collective-permute-start.3) | collective-permute-done | bytes 98336 | tf_op jit(solution)/shard_map/ppermute | solution.py:31
  14.3 1.2 %shard_map.67 = (bf16[40,256]{1,0:T(8,128)(2,1)S(1)}, bf16[40,256]{1,0:T(8,128)(2,1)S(1)}) custom-call(bf16[8,6144]{1,0:T(8,128)(2,1)S(1)} %copy-done.3, bf16[8,6144]{1,0:T(8,128)(2,1)S(1)} %collective-permute-done.refs_1_, bf16[4,7680]{1,0:T(4,128)(2,1)S(1)} %collective-permute-done.1.refs_2_, bf16[4,7680]{1,0:T(4,128)(2,1)S(1)} %collective-permute-done.2.refs_3_, ...), custom_call_target="tpu_custom_call" | custom-call | tf_op jit(solution)/shard_map/pallas_call | solution.py:283
  15.9 1.3 %collective-permute-start.8 = (s32[2,8]{1,0:T(2,128)S(1)}, s32[2,8]{1,0:T(2,128)S(1)}, u32[]{:S(2)}, u32[]{:S(2)}) collective-permute-start(s32[2,8]{1,0:T(2,128)S(1)} %shard_map.68), channel_id=1, source_target_pairs={{0,4},{1,13},{2,6},{3,15},{4,0},{5,9},{6,2},{7,11},{8,12},{9,5},{1... | collective-permute-start | bytes 200 | tf_op jit(solution)/shard_map/ppermute | solution.py:31
  17.2 2.3 %collective-permute-done.8.refs_0_ = s32[2,8]{1,0:T(2,128)S(1)} collective-permute-done((s32[2,8]{1,0:T(2,128)S(1)}, s32[2,8]{1,0:T(2,128)S(1)}, u32[]{:S(2)}, u32[]{:S(2)}) %collective-permute-start.8) | collective-permute-done | bytes 96 | tf_op jit(solution)/shard_map/ppermute | solution.py:31
  19.5 0.7 %shard_map.70.begun = f32[40,6144]{1,0:T(8,128)S(1)} custom-call(bf16[40,256]{1,0:T(8,128)(2,1)S(1)} %get-tuple-element.23.mine, bf16[8,8]{1,0:T(8,128)(2,1)S(1)} %shard_map.69.picks, bf16[1,256,6144]{2,1,0:T(8,128)(2,1)S(1)} %copy-done.2), custom_call_target="tpu_custom_call" | custom-call | tf_op jit(solution)/shard_map/pallas_call | solution.py:289
  20.3 0.8 %shard_map.71 = (bf16[4,7680]{1,0:T(4,128)(2,1)S(1)}, bf16[4,7680]{1,0:T(4,128)(2,1)S(1)}, bf16[4,7680]{1,0:T(4,128)(2,1)S(1)}, bf16[8,3072]{1,0:T(8,128)(2,1)S(1)}, f32[8,3072]{1,0:T(8,128)S(1)}) custom-call(bf16[40,256]{1,0:T(8,128)(2,1)S(1)} %collective-permute-done.7.theirs, bf16[8,8]{1,0:T(8,128)(2,1)S(1)} %shard_map.69.picks, ...), custom_call_target="tpu_custom_call" | custom-call | tf_op jit(solution)/shard_map/pallas_call | solution.py:293
  21.1 1.4 %collective-permute-start.10 = (bf16[4,7680]{1,0:T(4,128)(2,1)S(1)}, bf16[4,7680]{1,0:T(4,128)(2,1)S(1)}, u32[]{:S(2)}, u32[]{:S(2)}) collective-permute-start(bf16[4,7680]{1,0:T(4,128)(2,1)S(1)} %get-tuple-element.25), channel_id=1, source_target_pairs={{0,4},{1,13},{2,6},{3,15},{4,0},{5,9},{6,2},{7,11},{8,12},{9,5},{1... | collective-permute-start | bytes 184328 | tf_op jit(solution)/shard_map/ppermute | solution.py:31
  22.4 1.8 %collective-permute-start.11 = (bf16[4,7680]{1,0:T(4,128)(2,1)S(1)}, bf16[4,7680]{1,0:T(4,128)(2,1)S(1)}, u32[]{:S(2)}, u32[]{:S(2)}) collective-permute-start(bf16[4,7680]{1,0:T(4,128)(2,1)S(1)} %get-tuple-element.26), channel_id=1, source_target_pairs={{0,10},{1,9},{2,8},{3,11},{4,14},{5,13},{6,12},{7,15},{8,2},{9,1},... | collective-permute-start | bytes 184328 | tf_op jit(solution)/shard_map/ppermute | solution.py:31
  24.2 1.4 %collective-permute-start.12 = (bf16[4,7680]{1,0:T(4,128)(2,1)S(1)}, bf16[4,7680]{1,0:T(4,128)(2,1)S(1)}, u32[]{:S(2)}, u32[]{:S(2)}) collective-permute-start(bf16[4,7680]{1,0:T(4,128)(2,1)S(1)} %get-tuple-element.27), channel_id=1, source_target_pairs={{0,6},{1,15},{2,4},{3,13},{4,2},{5,11},{6,0},{7,9},{8,14},{9,7},{1... | collective-permute-start | bytes 184328 | tf_op jit(solution)/shard_map/ppermute | solution.py:31
  25.8 0.3 shard_map.64
  26.1 0.6 %collective-permute-start.14 = (bf16[8,3072]{1,0:T(8,128)(2,1)S(1)}, bf16[8,3072]{1,0:T(8,128)(2,1)S(1)}, u32[]{:S(2)}, u32[]{:S(2)}) collective-permute-start(bf16[8,3072]{1,0:T(8,128)(2,1)S(1)} %get-tuple-element.30), channel_id=1, source_target_pairs={{0,2},{1,3},{2,0},{3,1},{4,6},{5,7},{6,4},{7,5},{8,10},{9,11},{10,... | collective-permute-start | bytes 147464 | tf_op jit(solution)/shard_map/ppermute | solution.py:31
  26.7 4.3 %collective-permute-done.11.refs_1_ = bf16[4,7680]{1,0:T(4,128)(2,1)S(1)} collective-permute-done((bf16[4,7680]{1,0:T(4,128)(2,1)S(1)}, bf16[4,7680]{1,0:T(4,128)(2,1)S(1)}, u32[]{:S(2)}, u32[]{:S(2)}) %collective-permute-start.11) | collective-permute-done | bytes 61472 | tf_op jit(solution)/shard_map/ppermute | solution.py:31
  31.2 0.3 shard_map.72
  31.7 1.1 %collective-permute-done.13.got = bf16[8,3072]{1,0:T(8,128)(2,1)S(1)} collective-permute-done((bf16[8,3072]{1,0:T(8,128)(2,1)S(1)}, bf16[8,3072]{1,0:T(8,128)(2,1)S(1)}, u32[]{:S(2)}, u32[]{:S(2)}) %collective-permute-start.13) | collective-permute-done | bytes 49184 | tf_op jit(solution)/shard_map/ppermute | solution.py:35
  32.8 0.7 %shard_map.73 = bf16[8,3072]{1,0:T(8,128)(2,1)} custom-call(f32[8,128]{1,0:T(8,128)S(1)} %get-tuple-element.18.weights, f32[8,3072]{1,0:T(8,128)S(1)} %get-tuple-element.28.keep, bf16[8,3072]{1,0:T(8,128)(2,1)S(1)} %collective-permute-done.13.got, bf16[8,3072]{1,0:T(8,128)(2,1)S(1)} %collective-permute-done.14.back_half), custom_call_target="tpu_custom_call" | custom-call | tf_op jit(solution)/shard_map/pallas_call | solution.py:308
  (30 shorter events, 1.1 us)
Async XLA Ops:
  0.0 3.2 %copy-start.3 = (bf16[8,6144]{1,0:T(8,128)(2,1)S(1)}, bf16[8,6144]{1,0:T(8,128)(2,1)}, u32[]{:S(2)}) copy-start(bf16[8,6144]{1,0:T(8,128)(2,1)} %refs_0_.1) | copy-start | bytes 294916
  0.0 3.2 %copy-start.4 = (s32[8,2]{0,1:T(2,128)S(1)}, s32[8,2]{0,1:T(2,128)}, u32[]{:S(2)}) copy-start(s32[8,2]{0,1:T(2,128)} %param.7) | copy-start | bytes 196
  0.0 14.3 %copy-start.1 = (bf16[1,6144,256]{2,1,0:T(8,128)(2,1)S(1)}, bf16[1,6144,256]{2,1,0:T(8,128)(2,1)}, u32[]{:S(2)}) copy-start(bf16[1,6144,256]{2,1,0:T(8,128)(2,1)} %refs_9_.1) | copy-start | bytes 9437188
  0.0 14.3 %copy-start = (bf16[1,6144,256]{2,1,0:T(8,128)(2,1)S(1)}, bf16[1,6144,256]{2,1,0:T(8,128)(2,1)}, u32[]{:S(2)}) copy-start(bf16[1,6144,256]{2,1,0:T(8,128)(2,1)} %refs_8_.1) | copy-start | bytes 9437188
  0.0 20.3 %collective-permute-start.9 = (bf16[1,256,6144]{2,1,0:T(8,128)(2,1)}, bf16[1,256,6144]{2,1,0:T(8,128)(2,1)S(1)}, u32[]{:S(2)}, u32[]{:S(2)}) collective-permute-start(bf16[1,256,6144]{2,1,0:T(8,128)(2,1)} %down.1), channel_id=1, source_target_pairs={{0,1},{1,0},{2,3},{3,2},{4,5},{5,4},{6,7},{7,6},{8,9},{9,8},{10,11... | collective-permute-start | bytes 9437192 | tf_op jit(solution)/shard_map/ppermute | solution.py:35
  0.6 8.8 %collective-permute-start = (bf16[8,6144]{1,0:T(8,128)(2,1)}, bf16[8,6144]{1,0:T(8,128)(2,1)S(1)}, u32[]{:S(2)}, u32[]{:S(2)}) collective-permute-start(bf16[8,6144]{1,0:T(8,128)(2,1)} %refs_0_.1), channel_id=1, source_target_pairs={{0,4},{1,13},{2,6},{3,15},{4,0},{5,9},{6,2},{7,11},{8,12},{9,5},{1... | collective-permute-start | bytes 294920 | tf_op jit(solution)/shard_map/ppermute | solution.py:31
  3.6 6.6 %collective-permute-start.1 = (bf16[4,7680]{1,0:T(4,128)(2,1)S(1)}, bf16[4,7680]{1,0:T(4,128)(2,1)S(1)}, u32[]{:S(2)}, u32[]{:S(2)}) collective-permute-start(bf16[4,7680]{1,0:T(4,128)(2,1)S(1)} %get-tuple-element.20), channel_id=1, source_target_pairs={{0,10},{1,9},{2,8},{3,11},{4,14},{5,13},{6,12},{7,15},{8,2},{9,1},... | collective-permute-start | bytes 184328 | tf_op jit(solution)/shard_map/ppermute | solution.py:31
  7.2 5.9 %collective-permute-start.2 = (bf16[4,7680]{1,0:T(4,128)(2,1)S(1)}, bf16[4,7680]{1,0:T(4,128)(2,1)S(1)}, u32[]{:S(2)}, u32[]{:S(2)}) collective-permute-start(bf16[4,7680]{1,0:T(4,128)(2,1)S(1)} %get-tuple-element.21), channel_id=1, source_target_pairs={{0,6},{1,15},{2,4},{3,13},{4,2},{5,11},{6,0},{7,9},{8,14},{9,7},{1... | collective-permute-start | bytes 184328 | tf_op jit(solution)/shard_map/ppermute | solution.py:31
  7.8 6.3 %collective-permute-start.3 = (bf16[8,6144]{1,0:T(8,128)(2,1)S(1)}, bf16[8,6144]{1,0:T(8,128)(2,1)S(1)}, u32[]{:S(2)}, u32[]{:S(2)}) collective-permute-start(bf16[8,6144]{1,0:T(8,128)(2,1)S(1)} %copy-done.3), channel_id=1, source_target_pairs={{0,2},{1,3},{2,0},{3,1},{4,6},{5,7},{6,4},{7,5},{8,10},{9,11},{10,... | collective-permute-start | bytes 294920 | tf_op jit(solution)/shard_map/ppermute | solution.py:31
  9.4 4.9 %collective-permute-start.4 = (bf16[8,6144]{1,0:T(8,128)(2,1)S(1)}, bf16[8,6144]{1,0:T(8,128)(2,1)S(1)}, u32[]{:S(2)}, u32[]{:S(2)}) collective-permute-start(bf16[8,6144]{1,0:T(8,128)(2,1)S(1)} %collective-permute-done.refs_1_), channel_id=1, source_target_pairs={{0,1},{1,0},{2,3},{3,2},{4,5},{5,4},{6,7},{7,6},{8,9},{9,8},{10,11... | collective-permute-start | bytes 294920 | tf_op jit(solution)/shard_map/ppermute | solution.py:35
  10.2 4.0 %collective-permute-start.5 = (bf16[4,7680]{1,0:T(4,128)(2,1)S(1)}, bf16[4,7680]{1,0:T(4,128)(2,1)S(1)}, u32[]{:S(2)}, u32[]{:S(2)}) collective-permute-start(bf16[4,7680]{1,0:T(4,128)(2,1)S(1)} %collective-permute-done.1.refs_2_), channel_id=1, source_target_pairs={{0,1},{1,0},{2,3},{3,2},{4,5},{5,4},{6,7},{7,6},{8,9},{9,8},{10,11... | collective-permute-start | bytes 184328 | tf_op jit(solution)/shard_map/ppermute | solution.py:35
  13.0 1.2 %collective-permute-start.6 = (bf16[4,7680]{1,0:T(4,128)(2,1)S(1)}, bf16[4,7680]{1,0:T(4,128)(2,1)S(1)}, u32[]{:S(2)}, u32[]{:S(2)}) collective-permute-start(bf16[4,7680]{1,0:T(4,128)(2,1)S(1)} %collective-permute-done.2.refs_3_), channel_id=1, source_target_pairs={{0,1},{1,0},{2,3},{3,2},{4,5},{5,4},{6,7},{7,6},{8,9},{9,8},{10,11... | collective-permute-start | bytes 184328 | tf_op jit(solution)/shard_map/ppermute | solution.py:35
  15.5 4.0 %copy-start.2 = (bf16[1,256,6144]{2,1,0:T(8,128)(2,1)S(1)}, bf16[1,256,6144]{2,1,0:T(8,128)(2,1)}, u32[]{:S(2)}) copy-start(bf16[1,256,6144]{2,1,0:T(8,128)(2,1)} %down.1) | copy-start | bytes 9437188
  15.6 4.7 %collective-permute-start.7 = (bf16[40,256]{1,0:T(8,128)(2,1)S(1)}, bf16[40,256]{1,0:T(8,128)(2,1)S(1)}, u32[]{:S(2)}, u32[]{:S(2)}) collective-permute-start(bf16[40,256]{1,0:T(8,128)(2,1)S(1)} %get-tuple-element.22), channel_id=1, source_target_pairs={{0,1},{1,0},{2,3},{3,2},{4,5},{5,4},{6,7},{7,6},{8,9},{9,8},{10,11... | collective-permute-start | bytes 61448 | tf_op jit(solution)/shard_map/ppermute | solution.py:35
  15.9 3.6 %collective-permute-start.8 = (s32[2,8]{1,0:T(2,128)S(1)}, s32[2,8]{1,0:T(2,128)S(1)}, u32[]{:S(2)}, u32[]{:S(2)}) collective-permute-start(s32[2,8]{1,0:T(2,128)S(1)} %shard_map.68), channel_id=1, source_target_pairs={{0,4},{1,13},{2,6},{3,15},{4,0},{5,9},{6,2},{7,11},{8,12},{9,5},{1... | collective-permute-start | bytes 200 | tf_op jit(solution)/shard_map/ppermute | solution.py:31
  19.5 6.2 %copy-start.5 = (f32[8,4]{0,1:T(4,128)S(1)}, f32[8,4]{0,1:T(4,128)}, u32[]{:S(2)}) copy-start(f32[8,4]{0,1:T(4,128)} %param.8) | copy-start | bytes 388
  21.1 5.7 %collective-permute-start.10 = (bf16[4,7680]{1,0:T(4,128)(2,1)S(1)}, bf16[4,7680]{1,0:T(4,128)(2,1)S(1)}, u32[]{:S(2)}, u32[]{:S(2)}) collective-permute-start(bf16[4,7680]{1,0:T(4,128)(2,1)S(1)} %get-tuple-element.25), channel_id=1, source_target_pairs={{0,4},{1,13},{2,6},{3,15},{4,0},{5,9},{6,2},{7,11},{8,12},{9,5},{1... | collective-permute-start | bytes 184328 | tf_op jit(solution)/shard_map/ppermute | solution.py:31
  22.4 8.6 %collective-permute-start.11 = (bf16[4,7680]{1,0:T(4,128)(2,1)S(1)}, bf16[4,7680]{1,0:T(4,128)(2,1)S(1)}, u32[]{:S(2)}, u32[]{:S(2)}) collective-permute-start(bf16[4,7680]{1,0:T(4,128)(2,1)S(1)} %get-tuple-element.26), channel_id=1, source_target_pairs={{0,10},{1,9},{2,8},{3,11},{4,14},{5,13},{6,12},{7,15},{8,2},{9,1},... | collective-permute-start | bytes 184328 | tf_op jit(solution)/shard_map/ppermute | solution.py:31
  24.2 7.0 %collective-permute-start.12 = (bf16[4,7680]{1,0:T(4,128)(2,1)S(1)}, bf16[4,7680]{1,0:T(4,128)(2,1)S(1)}, u32[]{:S(2)}, u32[]{:S(2)}) collective-permute-start(bf16[4,7680]{1,0:T(4,128)(2,1)S(1)} %get-tuple-element.27), channel_id=1, source_target_pairs={{0,6},{1,15},{2,4},{3,13},{4,2},{5,11},{6,0},{7,9},{8,14},{9,7},{1... | collective-permute-start | bytes 184328 | tf_op jit(solution)/shard_map/ppermute | solution.py:31
  26.1 5.5 %collective-permute-start.14 = (bf16[8,3072]{1,0:T(8,128)(2,1)S(1)}, bf16[8,3072]{1,0:T(8,128)(2,1)S(1)}, u32[]{:S(2)}, u32[]{:S(2)}) collective-permute-start(bf16[8,3072]{1,0:T(8,128)(2,1)S(1)} %get-tuple-element.30), channel_id=1, source_target_pairs={{0,2},{1,3},{2,0},{3,1},{4,6},{5,7},{6,4},{7,5},{8,10},{9,11},{10,... | collective-permute-start | bytes 147464 | tf_op jit(solution)/shard_map/ppermute | solution.py:31
  31.5 1.3 %collective-permute-start.13 = (bf16[8,3072]{1,0:T(8,128)(2,1)S(1)}, bf16[8,3072]{1,0:T(8,128)(2,1)S(1)}, u32[]{:S(2)}, u32[]{:S(2)}) collective-permute-start(bf16[8,3072]{1,0:T(8,128)(2,1)S(1)} %get-tuple-element.29), channel_id=1, source_target_pairs={{0,1},{1,0},{2,3},{3,2},{4,5},{5,4},{6,7},{7,6},{8,9},{9,8},{10,11... | collective-permute-start | bytes 147464 | tf_op jit(solution)/shard_map/ppermute | solution.py:35
